TPU v7x, 1024 devices: a whole 4x4x32 slice. The times are simulated.
1024 devices in a mesh: gx: 4 (over y), gy: 4 (over z_hi), gz: 64 (over x, z_lo, core).
Axes of the slice: x: 4, y: 4, z: 32 (z_hi: 4, z_lo: 8; z = z_hi * 8 + z_lo), core: 2. Of those that a mesh axis runs over, the one named last changes fastest.
Arguments:
- section: float32 [25, 128, 64, 512], P(None, 'gz', 'gy', 'gx'), may hold values from -0.4 to 1.4, as said below
- base: float32 [25, 128, 64, 512], P(None, 'gz', 'gy', 'gx'), may hold values from -0.4 to 1.4, as said below
- accum: float32 [25, 128, 64, 512], P(None, 'gz', 'gy', 'gx'), may hold values from -4 to 4
Outputs:
- next_section: float32 [25, 128, 64, 512], P(None, 'gz', 'gy', 'gx')
- next_accum: float32 [25, 128, 64, 512], P(None, 'gz', 'gy', 'gx')
- slab: float32 [25, 128, 64, 512], P(None, 'gz')
Inputs may be any that keep to these rules, and one draw needn't show every extreme that they name: `section`: fields 0 and 17 (conformal factor and lapse) lie in 0.6 to 1.4; fields 1, 4 and 6 (the metric's diagonal) lie within 0.4 of 1; all other fields lie within 0.4 of 0. `base`: fields 0 and 17 (conformal factor and lapse) lie in 0.6 to 1.4; fields 1, 4 and 6 (the metric's diagonal) lie within 0.4 of 1; all other fields lie within 0.4 of 0.
All inputs are finite; a program needn't handle non-finite values.
Results may differ from a plain program's by a relative error of at most 0.0003.
Values sent between devices are 32-bit elements; how exact they have to be, the bound alone decides.
No kernel may reach another device: no remote copies, remote signals or barrier semaphores. Data moves between devices by JAX's collectives and lax.ppermute only.
A program may use at most 64 MiB of HBM per device.

v0:
```python
import jax
import jax.numpy as jnp
from jax import lax
from jax.sharding import PartitionSpec as P

STEP_DT = 0.25
SPACING = 1.0
DISSIPATE = 0.1
DRIVER_ETA = 2.0
KAPPA_ONE = 0.1
FIRST_TAPS = (1.0 / 12.0, -8.0 / 12.0, 0.0, 8.0 / 12.0, -1.0 / 12.0)
SECOND_TAPS = (-1.0 / 12.0, 16.0 / 12.0, -30.0 / 12.0, 16.0 / 12.0, -1.0 / 12.0)
FOURTH_TAPS = (1.0, -4.0, 6.0, -4.0, 1.0)
PAIR_SLOT = ((0, 1, 2), (1, 3, 4), (2, 4, 5))
PAIR_LIST = ((0, 0), (0, 1), (0, 2), (1, 1), (1, 2), (2, 2))


def extended(block, sides, width):
    for axis, dim in sides:
        count = lax.axis_size(axis)
        forward = [(i, i + 1) for i in range(count - 1)]
        forward.append((count - 1, 0))
        backward = [(target, source) for source, target in forward]
        low = lax.ppermute(
            lax.slice_in_dim(block, block.shape[dim] - width, None, axis=dim), axis, forward
        )
        high = lax.ppermute(lax.slice_in_dim(block, 0, width, axis=dim), axis, backward)
        block = jnp.concatenate([low, block, high], axis=dim)
    return block


def whole_of(array, axes, dim):
    result = array
    for number in range(len(axes) - 1, -1, -1):
        result = lax.all_gather(result, axes[number], axis=dim, tiled=True)
    return result


def window(padded, shifts):
    interior = (padded.shape[1] - 4, padded.shape[2] - 4, padded.shape[3] - 4)
    corner = (2 + shifts[2], 2 + shifts[1], 2 + shifts[0])
    return padded[
        :,
        corner[0] : corner[0] + interior[0],
        corner[1] : corner[1] + interior[1],
        corner[2] : corner[2] + interior[2],
    ]


def moved(direction, amount):
    shifts = [0, 0, 0]
    shifts[direction] = amount
    return shifts


def line_sum(padded, direction, weights):
    running = None
    for position in range(5):
        if weights[position] != 0.0:
            weighted = weights[position] * window(padded, moved(direction, position - 2))
            running = weighted if running is None else running + weighted
    return running


def cross_sum(padded, first_dir, second_dir):
    running = None
    for first_pos in range(5):
        for second_pos in range(5):
            factor = FIRST_TAPS[first_pos] * FIRST_TAPS[second_pos]
            if factor != 0.0:
                shifts = [0, 0, 0]
                shifts[first_dir] = first_pos - 2
                shifts[second_dir] = second_pos - 2
                weighted = factor * window(padded, shifts)
                running = weighted if running is None else running + weighted
    return running


def evolve_rate(padded):
    centre = window(padded, (0, 0, 0))
    gradients = [line_sum(padded, direction, FIRST_TAPS) / SPACING for direction in range(3)]
    curves = [
        line_sum(padded, direction, SECOND_TAPS) / (SPACING * SPACING) for direction in range(3)
    ]
    smoothing = (
        line_sum(padded, 0, FOURTH_TAPS)
        + line_sum(padded, 1, FOURTH_TAPS)
        + line_sum(padded, 2, FOURTH_TAPS)
    )
    chosen = jnp.concatenate([padded[0:1], padded[17:21]], axis=0)
    mixed_terms = {}
    for dir_pair in ((0, 1), (0, 2), (1, 2)):
        mixed_terms[dir_pair] = cross_sum(chosen, dir_pair[0], dir_pair[1]) / (SPACING * SPACING)

    def second_of(chosen_slot, field_slot, axis_one, axis_two):
        if axis_one == axis_two:
            return curves[axis_one][field_slot]
        return mixed_terms[min(axis_one, axis_two), max(axis_one, axis_two)][chosen_slot]

    def metric_of(axis_one, axis_two):
        return centre[1 + PAIR_SLOT[axis_one][axis_two]]

    def traceless_of(axis_one, axis_two):
        return centre[8 + PAIR_SLOT[axis_one][axis_two]]

    def inverse_of(axis_one, axis_two):
        return (2.0 if axis_one == axis_two else 0.0) - metric_of(axis_one, axis_two)

    def advect(field_slot):
        return (
            centre[18] * gradients[0][field_slot]
            + centre[19] * gradients[1][field_slot]
            + centre[20] * gradients[2][field_slot]
        )

    conformal = centre[0]
    trace_curv = centre[7]
    lapse_field = centre[17]
    theta_field = centre[24]
    divergence = gradients[0][18] + gradients[1][19] + gradients[2][20]
    lap_conformal = curves[0][0] + curves[1][0] + curves[2][0]
    squares_a = sum(
        (traceless_of(axis_one, axis_two) ** 2 for axis_one in range(3) for axis_two in range(3))
    )

    def lapse_dd(axis_one, axis_two):
        return second_of(1, 17, axis_one, axis_two)

    ricci_table = []
    for axis_one, axis_two in PAIR_LIST:
        field_slot = 1 + PAIR_SLOT[axis_one][axis_two]
        flat_part = curves[0][field_slot] + curves[1][field_slot] + curves[2][field_slot]
        conformal_part = second_of(0, 0, axis_one, axis_two) + (
            lap_conformal if axis_one == axis_two else 0.0
        )
        ricci_table.append(
            -0.5 * flat_part
            + 0.5 * (gradients[axis_one][14 + axis_two] + gradients[axis_two][14 + axis_one])
            + conformal_part / (2.0 * conformal)
        )

    def ricci_of(axis_one, axis_two):
        return ricci_table[PAIR_SLOT[axis_one][axis_two]]

    ricci_scalar = conformal * sum(
        (
            inverse_of(axis_one, axis_two) * ricci_of(axis_one, axis_two)
            for axis_one in range(3)
            for axis_two in range(3)
        )
    )
    lapse_trace = sum(
        (
            inverse_of(axis_one, axis_two) * lapse_dd(axis_one, axis_two)
            for axis_one in range(3)
            for axis_two in range(3)
        )
    )
    rates = [None] * 25
    rates[0] = advect(0) + 2.0 / 3.0 * conformal * (lapse_field * trace_curv - divergence)
    for axis_one, axis_two in PAIR_LIST:
        field_slot = PAIR_SLOT[axis_one][axis_two]
        lie_part = sum(
            (
                metric_of(axis_one, axis_sum) * gradients[axis_two][18 + axis_sum]
                + metric_of(axis_two, axis_sum) * gradients[axis_one][18 + axis_sum]
                for axis_sum in range(3)
            )
        )
        rates[1 + field_slot] = (
            advect(1 + field_slot)
            - 2.0 * lapse_field * traceless_of(axis_one, axis_two)
            + lie_part
            - 2.0 / 3.0 * metric_of(axis_one, axis_two) * divergence
        )
    rates[7] = (
        advect(7)
        - conformal * lapse_trace
        + lapse_field * (squares_a + trace_curv * trace_curv / 3.0)
        + KAPPA_ONE * lapse_field * theta_field
    )

    def source_of(axis_one, axis_two):
        return -lapse_dd(axis_one, axis_two) + lapse_field * ricci_of(axis_one, axis_two)

    trace_part = sum(
        (
            inverse_of(axis_one, axis_two) * source_of(axis_one, axis_two)
            for axis_one in range(3)
            for axis_two in range(3)
        )
    )
    for axis_one, axis_two in PAIR_LIST:
        field_slot = PAIR_SLOT[axis_one][axis_two]
        free_part = source_of(axis_one, axis_two) - metric_of(axis_one, axis_two) * trace_part / 3.0
        product_part = sum(
            (
                traceless_of(axis_one, axis_sum) * traceless_of(axis_sum, axis_two)
                for axis_sum in range(3)
            )
        )
        lie_part = sum(
            (
                traceless_of(axis_one, axis_sum) * gradients[axis_two][18 + axis_sum]
                + traceless_of(axis_two, axis_sum) * gradients[axis_one][18 + axis_sum]
                for axis_sum in range(3)
            )
        )
        rates[8 + field_slot] = (
            advect(8 + field_slot)
            + conformal * free_part
            + lapse_field * (trace_curv * traceless_of(axis_one, axis_two) - 2.0 * product_part)
            + lie_part
            - 2.0 / 3.0 * traceless_of(axis_one, axis_two) * divergence
        )
    for axis_one in range(3):
        gauge_part = (
            -2.0
            * sum(
                (
                    traceless_of(axis_one, axis_two) * gradients[axis_two][17]
                    for axis_two in range(3)
                )
            )
            + 2.0
            * lapse_field
            * (
                -(2.0 / 3.0)
                * sum(
                    (
                        inverse_of(axis_one, axis_two) * gradients[axis_two][7]
                        for axis_two in range(3)
                    )
                )
                - 1.5
                * sum(
                    (
                        traceless_of(axis_one, axis_two) * gradients[axis_two][0]
                        for axis_two in range(3)
                    )
                )
                / conformal
            )
            + curves[0][18 + axis_one]
            + curves[1][18 + axis_one]
            + curves[2][18 + axis_one]
            + sum(
                (
                    second_of(2 + axis_two, 18 + axis_two, axis_one, axis_two)
                    for axis_two in range(3)
                )
            )
            / 3.0
            + 2.0 / 3.0 * centre[14 + axis_one] * divergence
            - sum(
                (
                    centre[14 + axis_two] * gradients[axis_two][18 + axis_one]
                    for axis_two in range(3)
                )
            )
        )
        rates[14 + axis_one] = advect(14 + axis_one) + gauge_part
        rates[18 + axis_one] = advect(18 + axis_one) + 0.75 * centre[21 + axis_one]
        rates[21 + axis_one] = (
            advect(21 + axis_one) + gauge_part - DRIVER_ETA * centre[21 + axis_one]
        )
    rates[17] = advect(17) - 2.0 * lapse_field * (trace_curv - 2.0 * theta_field)
    rates[24] = (
        advect(24)
        + 0.5 * lapse_field * (ricci_scalar + 2.0 / 3.0 * trace_curv * trace_curv - squares_a)
        - 2.0 * KAPPA_ONE * lapse_field * theta_field
    )
    return jnp.stack(rates, axis=0) + -DISSIPATE / 16.0 * smoothing


def shards(section, base, accum):
    padded = extended(section, (("gx", 3), ("gy", 2), ("gz", 1)), 2)
    rates = evolve_rate(padded)
    next_section = base + 0.5 * STEP_DT * rates
    next_accum = accum + STEP_DT / 3.0 * rates
    stacked = whole_of(next_section[None], ("gx", "gy"), 0)
    width_parts = lax.axis_size("gx")
    height_parts = lax.axis_size("gy")
    fields_count, planes, block_rows, block_cols = next_section.shape
    regrouped = stacked.reshape(
        width_parts, height_parts, fields_count, planes, block_rows, block_cols
    )
    regrouped = jnp.transpose(regrouped, (2, 3, 1, 4, 0, 5))
    slab = regrouped.reshape(
        fields_count, planes, height_parts * block_rows, width_parts * block_cols
    )
    return (next_section, next_accum, slab)


def solution(mesh):
    return jax.shard_map(
        shards,
        mesh=mesh,
        in_specs=(P(None, "gz", "gy", "gx"), P(None, "gz", "gy", "gx"), P(None, "gz", "gy", "gx")),
        out_specs=(P(None, "gz", "gy", "gx"), P(None, "gz", "gy", "gx"), P(None, "gz", None, None)),
        check_vma=False,
    )
```

profile of v0, /device:TPU:1, one launch (start us, length us, event | category | flops | bytes accessed | tf_op | source)
XLA Modules:
  0.0 360.2 jit_solution(8115456881223873816)
XLA Ops:
  7.2 1.3 fusion.195
  8.6 4.0 %collective-permute-start = (f32[25,2,16,2]{3,2,1,0:T(8,128)S(1)}, f32[25,2,16,2]{3,2,1,0:T(8,128)S(1)}, u32[]{:S(2)}, u32[]{:S(2)}) collective-permute-start(f32[25,2,16,2]{3,2,1,0:T(8,128)S(1)} %get-tuple-element.39), channel_id=1, source_target_pairs={{0,256},{256,512},{512,768},{768,0},{1,257},{257,513},{513,769},{7... | collective-permute-start | bytes 19208 | tf_op jit(solution)/shard_map/ppermute | solution.py:24
  12.6 3.4 collective-permute-start.1
  16.0 3.4 collective-permute-done
  19.4 1.9 collective-permute-done.1
  21.7 18.7 %collective-permute-start.2 = (f32[25,2,2,132]{3,2,1,0:T(2,128)S(1)}, f32[25,2,2,132]{3,2,1,0:T(2,128)S(1)}, u32[]{:S(2)}, u32[]{:S(2)}) collective-permute-start(f32[25,2,2,132]{3,2,1,0:T(2,128)S(1)} %get-tuple-element.36), channel_id=1, source_target_pairs={{0,64},{64,128},{128,192},{192,0},{1,65},{65,129},{129,193},{193,1... | collective-permute-start | bytes 158408 | tf_op jit(solution)/shard_map/ppermute | solution.py:24
  40.4 9.2 %collective-permute-start.3 = (f32[25,2,2,132]{3,2,1,0:T(2,128)S(1)}, f32[25,2,2,132]{3,2,1,0:T(2,128)S(1)}, u32[]{:S(2)}, u32[]{:S(2)}) collective-permute-start(f32[25,2,2,132]{3,2,1,0:T(2,128)S(1)} %get-tuple-element.37), channel_id=1, source_target_pairs={{64,0},{128,64},{192,128},{0,192},{65,1},{129,65},{193,129},{1,193... | collective-permute-start | bytes 158408 | tf_op jit(solution)/shard_map/ppermute | solution.py:27
  49.6 0.7 collective-permute-done.2
  50.3 23.5 %collective-permute-done.3 = f32[25,2,2,132]{3,2,1,0:T(2,128)S(1)} collective-permute-done((f32[25,2,2,132]{3,2,1,0:T(2,128)S(1)}, f32[25,2,2,132]{3,2,1,0:T(2,128)S(1)}, u32[]{:S(2)}, u32[]{:S(2)}) %collective-permute-start.3) | collective-permute-done | bytes 52832 | tf_op jit(solution)/shard_map/ppermute | solution.py:27
  73.8 0.6 pad_maximum_fusion
  74.9 3.0 collective-permute-start.5
  77.9 2.6 collective-permute-start.4
  80.5 0.7 add_add_fusion.1
  81.4 10.8 %collective-permute-done.5 = f32[25,2,20,132]{3,1,2,0:T(2,128)S(1)} collective-permute-done((f32[25,2,20,132]{3,1,2,0:T(2,128)S(1)}, f32[25,2,20,132]{3,1,2,0:T(2,128)S(1)}, u32[]{:S(2)}, u32[]{:S(2)}) %collective-permute-start.5) | collective-permute-done | bytes 528032 | tf_op jit(solution)/shard_map/ppermute | solution.py:27
  92.4 8.2 %collective-permute-done.4 = f32[25,2,20,132]{3,1,2,0:T(2,128)S(1)} collective-permute-done((f32[25,2,20,132]{3,1,2,0:T(2,128)S(1)}, f32[25,2,20,132]{3,1,2,0:T(2,128)S(1)}, u32[]{:S(2)}, u32[]{:S(2)}) %collective-permute-start.4) | collective-permute-done | bytes 528032 | tf_op jit(solution)/shard_map/ppermute | solution.py:24
  102.0 0.6 add_add_fusion
  102.6 0.9 add_add_fusion.2
  104.5 0.7 copy-done.1
  105.2 1.6 multiply_add_fusion
  106.8 0.8 multiply_add_fusion.1
  107.9 143.9 %all-gather.6.cloned.1.call-done = f32[100,2,16,128]{3,2,1,0:T(8,128)} async-done(((f32[25,2,16,128]{3,2,1,0:T(8,128)}), f32[100,2,16,128]{3,2,1,0:T(8,128)}) %all-gather.6.cloned.1.call-update) | async-done | bytes 1638416 | tf_op jit(solution)/shard_map/all_gather | solution.py:35
  251.8 82.3 %all-gather.4.cloned.1.call-done = f32[16,25,2,16,128]{4,3,2,1,0:T(8,128)} async-done(((f32[4,25,2,16,128]{4,3,2,1,0:T(8,128)}), f32[16,25,2,16,128]{4,3,2,1,0:T(8,128)}) %all-gather.4.cloned.1.call-update) | async-done | bytes 6553616 | tf_op jit(solution)/shard_map/all_gather | solution.py:35
  334.1 10.8 %copy.54 = f32[25,2,4,16,4,128]{5,4,3,2,1,0:T(4,128)} copy(f32[25,2,4,16,4,128]{5,3,1,0,2,4:T(8,128)} %bitcast.4) | data formatting | bytes 13107200 | tf_op jit(solution)/shard_map/transpose | solution.py:288
  344.9 8.5 %reshape.13 = f32[25,2,64,512]{3,2,1,0:T(8,128)} reshape(f32[25,2,4,16,4,128]{5,4,3,2,1,0:T(4,128)} %copy.54) | data formatting | bytes 13107200 | tf_op jit(solution)/shard_map/reshape | solution.py:289
  (44 shorter events, 3.8 us)
Async XLA Ops:
  7.2 14.1 %copy-start = (f32[25,2,16,128]{3,2,1,0:T(8,128)S(1)}, f32[25,2,16,128]{3,2,1,0:T(8,128)}, u32[]{:S(2)}) copy-start(f32[25,2,16,128]{3,2,1,0:T(8,128)} %param.3) | copy-start | bytes 1228804
  7.2 244.6 %all-gather.6.cloned.1.call-start = ((), (), s32[]{:S(2)}) async-start(), calls=%async_computation.1 | async-start | bytes 2048000 | tf_op jit(solution)/shard_map/all_gather | solution.py:35
  8.6 10.8 %collective-permute-start = (f32[25,2,16,2]{3,2,1,0:T(8,128)S(1)}, f32[25,2,16,2]{3,2,1,0:T(8,128)S(1)}, u32[]{:S(2)}, u32[]{:S(2)}) collective-permute-start(f32[25,2,16,2]{3,2,1,0:T(8,128)S(1)} %get-tuple-element.39), channel_id=1, source_target_pairs={{0,256},{256,512},{512,768},{768,0},{1,257},{257,513},{513,769},{7... | collective-permute-start | bytes 19208 | tf_op jit(solution)/shard_map/ppermute | solution.py:24
  12.6 8.7 %collective-permute-start.1 = (f32[25,2,16,2]{3,2,1,0:T(8,128)S(1)}, f32[25,2,16,2]{3,2,1,0:T(8,128)S(1)}, u32[]{:S(2)}, u32[]{:S(2)}) collective-permute-start(f32[25,2,16,2]{3,2,1,0:T(8,128)S(1)} %get-tuple-element.40), channel_id=1, source_target_pairs={{256,0},{512,256},{768,512},{0,768},{257,1},{513,257},{769,513},{1... | collective-permute-start | bytes 19208 | tf_op jit(solution)/shard_map/ppermute | solution.py:27
  21.7 28.6 %collective-permute-start.2 = (f32[25,2,2,132]{3,2,1,0:T(2,128)S(1)}, f32[25,2,2,132]{3,2,1,0:T(2,128)S(1)}, u32[]{:S(2)}, u32[]{:S(2)}) collective-permute-start(f32[25,2,2,132]{3,2,1,0:T(2,128)S(1)} %get-tuple-element.36), channel_id=1, source_target_pairs={{0,64},{64,128},{128,192},{192,0},{1,65},{65,129},{129,193},{193,1... | collective-permute-start | bytes 158408 | tf_op jit(solution)/shard_map/ppermute | solution.py:24
  40.4 33.4 %collective-permute-start.3 = (f32[25,2,2,132]{3,2,1,0:T(2,128)S(1)}, f32[25,2,2,132]{3,2,1,0:T(2,128)S(1)}, u32[]{:S(2)}, u32[]{:S(2)}) collective-permute-start(f32[25,2,2,132]{3,2,1,0:T(2,128)S(1)} %get-tuple-element.37), channel_id=1, source_target_pairs={{64,0},{128,64},{192,128},{0,192},{65,1},{129,65},{193,129},{1,193... | collective-permute-start | bytes 158408 | tf_op jit(solution)/shard_map/ppermute | solution.py:27
  74.9 17.3 %collective-permute-start.5 = (f32[25,2,20,132]{3,1,2,0:T(2,128)S(1)}, f32[25,2,20,132]{3,1,2,0:T(2,128)S(1)}, u32[]{:S(2)}, u32[]{:S(2)}) collective-permute-start(f32[25,2,20,132]{3,1,2,0:T(2,128)S(1)} %copy.46), channel_id=1, source_target_pairs={{1,0},{2,1},{3,2},{4,3},{5,4},{6,5},{7,6},{8,7},{9,8},{10,9},{11,1... | collective-permute-start | bytes 1584008 | tf_op jit(solution)/shard_map/ppermute | solution.py:27
  77.9 22.7 %collective-permute-start.4 = (f32[25,2,20,132]{3,1,2,0:T(2,128)S(1)}, f32[25,2,20,132]{3,1,2,0:T(2,128)S(1)}, u32[]{:S(2)}, u32[]{:S(2)}) collective-permute-start(f32[25,2,20,132]{3,1,2,0:T(2,128)S(1)} %copy.46), channel_id=1, source_target_pairs={{0,1},{1,2},{2,3},{3,4},{4,5},{5,6},{6,7},{7,8},{8,9},{9,10},{10,1... | collective-permute-start | bytes 1584008 | tf_op jit(solution)/shard_map/ppermute | solution.py:24
  104.2 1.0 copy-start.1
  105.2 1.6 copy-start.2
  107.6 226.5 %all-gather.4.cloned.1.call-start = ((), (), s32[]{:S(2)}) async-start(), calls=%async_computation | async-start | bytes 8192000 | tf_op jit(solution)/shard_map/all_gather | solution.py:35
Sparse Core Ops, SparseCore 0:
  107.8 143.9 all-gather.5
  254.4 79.6 all-gather.3
where the time goes:
time: 361 us; the launch traced here: 360 us
  waiting for transfers between devices  275 us (76%)
  starting transfers between devices  41.1 us (11%)
  local copies, waits for them, and re-layouts  22.2 us (6%)
  between operations  14.3 us (4%)
  other arithmetic  7.84 us (2%)
    all_gather x2, waiting for transfers between devices, whole_of(): result = lax.all_gather(result, axes[number], axis=dim, tiled=True)  226 us
    ppermute x3, waiting for transfers between devices, extended(): lax.ppermute(lax.slice_in_dim(block, 0, width, axis=dim), axis, backward)  36.2 us
    ppermute x3, starting transfers between devices, extended(): lax.ppermute(lax.slice_in_dim(block, block.shape[dim] - width, None, axis...  25.3 us
    ppermute x3, starting transfers between devices, extended(): lax.ppermute(lax.slice_in_dim(block, 0, width, axis=dim), axis, backward)  15.5 us
    ppermute x3, waiting for transfers between devices, extended(): lax.ppermute(lax.slice_in_dim(block, block.shape[dim] - width, None, axis...  12.3 us
    transpose x1, local copies, waits for them, and re-layouts, shards(): regrouped = jnp.transpose(regrouped, (2, 3, 1, 4, 0, 5))  10.8 us
    reshape x1, local copies, waits for them, and re-layouts, shards(): regrouped.reshape(fields_count, planes, height_parts * block_rows, width_...  8.47 us
  transfers between devices with their start and end apart: 8, of which 8 were waited for; matrix products, arithmetic and copies ran while one was open for 0% of the time, Pallas kernels for 0%

commit v1 on v0

--- a/solution.py
+++ b/solution.py
@@ -1,7 +1,10 @@
 import jax
 import jax.numpy as jnp
 from jax import lax
+from jax.experimental import pallas as pl
+from jax.experimental.pallas import tpu as pltpu
 from jax.sharding import PartitionSpec as P
+
 
 STEP_DT = 0.25
 SPACING = 1.0
@@ -27,13 +30,6 @@
         high = lax.ppermute(lax.slice_in_dim(block, 0, width, axis=dim), axis, backward)
         block = jnp.concatenate([low, block, high], axis=dim)
     return block
-
-
-def whole_of(array, axes, dim):
-    result = array
-    for number in range(len(axes) - 1, -1, -1):
-        result = lax.all_gather(result, axes[number], axis=dim, tiled=True)
-    return result
 
 
 def window(padded, shifts):
@@ -273,30 +269,110 @@
     return jnp.stack(rates, axis=0) + -DISSIPATE / 16.0 * smoothing
 
 
+AXES = ("gx", "gy", "gz")
+N_GX = 4
+N_GY = 4
+
+
+def turned(axis, sense):
+    pairs = []
+    size_z = lax.axis_size("gz")
+    for col in range(N_GX):
+        for row in range(N_GY):
+            for deep in range(size_z):
+                step = sense if deep % 2 == 0 else -sense
+                to_col = (col + step) % N_GX if axis == "gx" else col
+                to_row = (row + step) % N_GY if axis == "gy" else row
+                pairs.append(
+                    ((col * N_GY + row) * size_z + deep, (to_col * N_GY + to_row) * size_z + deep)
+                )
+    return pairs
+
+
+def place_kernel(step_y, *refs):
+    own, first, second, back, slab, sems = refs[0], refs[1], refs[2], refs[3], refs[-2], refs[-1]
+    sense = 1 - 2 * lax.rem(lax.axis_index("gz"), 2)
+    row = lax.rem(lax.axis_index("gy") - sense * step_y + 2 * N_GY, N_GY)
+    height, width = own.shape[2], own.shape[3]
+    copies = []
+    for number, (piece, away) in enumerate(((own, 0), (first, 1), (second, 2), (back, -1))):
+        col = lax.rem(lax.axis_index("gx") - sense * away + 2 * N_GX, N_GX)
+        copies.append(
+            pltpu.make_async_copy(
+                piece,
+                slab.at[
+                    :,
+                    :,
+                    pl.ds(pl.multiple_of(row * height, height), height),
+                    pl.ds(pl.multiple_of(col * width, width), width),
+                ],
+                sems.at[number],
+            )
+        )
+    for copy in copies:
+        copy.start()
+    for copy in copies:
+        copy.wait()
+
+
+def placed(slab, pieces, step_y):
+    fields_count, planes, height, width = pieces[0].shape
+    shape = jax.ShapeDtypeStruct((fields_count, planes, N_GY * height, N_GX * width), jnp.float32)
+    args = list(pieces)
+    specs = [pl.BlockSpec(memory_space=pltpu.VMEM)] * 4
+    aliases = {}
+    if slab is not None:
+        args.append(slab)
+        specs.append(pl.BlockSpec(memory_space=pl.ANY))
+        aliases = {4: 0}
+    return pl.pallas_call(
+        lambda *refs: place_kernel(step_y, *refs),
+        out_shape=shape,
+        in_specs=specs,
+        out_specs=pl.BlockSpec(memory_space=pl.ANY),
+        scratch_shapes=[pltpu.SemaphoreType.DMA((4,))],
+        input_output_aliases=aliases,
+        cost_estimate=pl.CostEstimate(flops=2000000, bytes_accessed=3300000, transcendentals=0),
+        compiler_params=pltpu.CompilerParams(vmem_limit_bytes=4 * 1024 * 1024),
+    )(*args)
+
+
+def slab_of(block):
+    along_y = turned("gy", 1)
+    along_x = turned("gx", 1)
+    against_x = turned("gx", -1)
+    slab = None
+    current = block
+    for step in range(4):
+        following = None
+        if step < 3:
+            following = lax.ppermute(current, AXES, along_y)
+        first = lax.ppermute(current, AXES, along_x)
+        back = lax.ppermute(current, AXES, against_x)
+        second = lax.ppermute(first, AXES, along_x)
+        if following is not None:
+            following, first, second, back = lax.optimization_barrier(
+                (following, first, second, back)
+            )
+        slab = placed(slab, (current, first, second, back), step)
+        current = following
+    return slab
+
+
 def shards(section, base, accum):
     padded = extended(section, (("gx", 3), ("gy", 2), ("gz", 1)), 2)
     rates = evolve_rate(padded)
     next_section = base + 0.5 * STEP_DT * rates
     next_accum = accum + STEP_DT / 3.0 * rates
-    stacked = whole_of(next_section[None], ("gx", "gy"), 0)
-    width_parts = lax.axis_size("gx")
-    height_parts = lax.axis_size("gy")
-    fields_count, planes, block_rows, block_cols = next_section.shape
-    regrouped = stacked.reshape(
-        width_parts, height_parts, fields_count, planes, block_rows, block_cols
-    )
-    regrouped = jnp.transpose(regrouped, (2, 3, 1, 4, 0, 5))
-    slab = regrouped.reshape(
-        fields_count, planes, height_parts * block_rows, width_parts * block_cols
-    )
-    return (next_section, next_accum, slab)
+    return (next_section, next_accum, slab_of(next_section))
 
 
 def solution(mesh):
+    split = P(None, "gz", "gy", "gx")
     return jax.shard_map(
         shards,
         mesh=mesh,
-        in_specs=(P(None, "gz", "gy", "gx"), P(None, "gz", "gy", "gx"), P(None, "gz", "gy", "gx")),
-        out_specs=(P(None, "gz", "gy", "gx"), P(None, "gz", "gy", "gx"), P(None, "gz", None, None)),
+        in_specs=(split, split, split),
+        out_specs=(split, split, P(None, "gz", None, None)),
         check_vma=False,
     )

time: 361 us -> 274 us (0.76)
  the two profiles are of different devices: /device:TPU:1 before, /device:TPU:66 now
where the time goes in v1:
time: 274 us; the launch traced here: 273 us
  starting transfers between devices  158 us (58%)
  waiting for transfers between devices  99.3 us (36%)
  other arithmetic  7.08 us (3%)
  Pallas kernels  4.83 us (2%)
  local copies, waits for them, and re-layouts  2.96 us (1%)
    ppermute x3, starting transfers between devices, slab_of(): following = lax.ppermute(current, AXES, along_y)  82.1 us
    ppermute x3, waiting for transfers between devices, slab_of(): following = lax.ppermute(current, AXES, along_y)  32 us
    ppermute x3, waiting for transfers between devices, extended(): lax.ppermute(lax.slice_in_dim(block, block.shape[dim] - width, None, axis...  24.7 us
    ppermute x3, waiting for transfers between devices, extended(): lax.ppermute(lax.slice_in_dim(block, 0, width, axis=dim), axis, backward)  21.1 us
    ppermute x3, starting transfers between devices, extended(): lax.ppermute(lax.slice_in_dim(block, block.shape[dim] - width, None, axis...  21.1 us
    ppermute x4, starting transfers between devices, slab_of(): back = lax.ppermute(current, AXES, against_x)  19 us
    ppermute x3, starting transfers between devices, extended(): lax.ppermute(lax.slice_in_dim(block, 0, width, axis=dim), axis, backward)  14.6 us
    ppermute x4, starting transfers between devices, slab_of(): first = lax.ppermute(current, AXES, along_x)  13 us
  transfers between devices with their start and end apart: 21, of which 14 were waited for; matrix products, arithmetic and copies ran while one was open for 0% of the time, Pallas kernels for 1%

profile of v1, /device:TPU:66, one launch (start us, length us, event | category | flops | bytes accessed | tf_op | source)
XLA Modules:
  0.0 273.0 jit_solution(3584010550645992053)
XLA Ops:
  2.0 3.5 %collective-permute-start = (f32[25,2,16,2]{3,2,1,0:T(8,128)S(1)}, f32[25,2,16,2]{3,2,1,0:T(8,128)S(1)}, u32[]{:S(2)}, u32[]{:S(2)}) collective-permute-start(f32[25,2,16,2]{3,2,1,0:T(8,128)S(1)} %get-tuple-element.60), channel_id=1, source_target_pairs={{0,256},{256,512},{512,768},{768,0},{1,257},{257,513},{513,769},{7... | collective-permute-start | bytes 19208 | tf_op jit(solution)/shard_map/ppermute | solution.py:27
  5.5 3.6 %collective-permute-start.1 = (f32[25,2,16,2]{3,2,1,0:T(8,128)S(1)}, f32[25,2,16,2]{3,2,1,0:T(8,128)S(1)}, u32[]{:S(2)}, u32[]{:S(2)}) collective-permute-start(f32[25,2,16,2]{3,2,1,0:T(8,128)S(1)} %get-tuple-element.61), channel_id=1, source_target_pairs={{256,0},{512,256},{768,512},{0,768},{257,1},{513,257},{769,513},{1... | collective-permute-start | bytes 19208 | tf_op jit(solution)/shard_map/ppermute | solution.py:30
  9.1 7.3 %collective-permute-done = f32[25,2,16,2]{3,2,1,0:T(8,128)S(1)} collective-permute-done((f32[25,2,16,2]{3,2,1,0:T(8,128)S(1)}, f32[25,2,16,2]{3,2,1,0:T(8,128)S(1)}, u32[]{:S(2)}, u32[]{:S(2)}) %collective-permute-start) | collective-permute-done | bytes 6432 | tf_op jit(solution)/shard_map/ppermute | solution.py:27
  18.7 15.7 %collective-permute-start.2 = (f32[25,2,2,132]{3,2,1,0:T(2,128)S(1)}, f32[25,2,2,132]{3,2,1,0:T(2,128)S(1)}, u32[]{:S(2)}, u32[]{:S(2)}) collective-permute-start(f32[25,2,2,132]{3,2,1,0:T(2,128)S(1)} %get-tuple-element.57), channel_id=1, source_target_pairs={{0,64},{64,128},{128,192},{192,0},{1,65},{65,129},{129,193},{193,1... | collective-permute-start | bytes 158408 | tf_op jit(solution)/shard_map/ppermute | solution.py:27
  34.5 7.4 %collective-permute-start.3 = (f32[25,2,2,132]{3,2,1,0:T(2,128)S(1)}, f32[25,2,2,132]{3,2,1,0:T(2,128)S(1)}, u32[]{:S(2)}, u32[]{:S(2)}) collective-permute-start(f32[25,2,2,132]{3,2,1,0:T(2,128)S(1)} %get-tuple-element.58), channel_id=1, source_target_pairs={{64,0},{128,64},{192,128},{0,192},{65,1},{129,65},{193,129},{1,193... | collective-permute-start | bytes 158408 | tf_op jit(solution)/shard_map/ppermute | solution.py:30
  41.9 8.0 %collective-permute-done.2 = f32[25,2,2,132]{3,2,1,0:T(2,128)S(1)} collective-permute-done((f32[25,2,2,132]{3,2,1,0:T(2,128)S(1)}, f32[25,2,2,132]{3,2,1,0:T(2,128)S(1)}, u32[]{:S(2)}, u32[]{:S(2)}) %collective-permute-start.2) | collective-permute-done | bytes 52832 | tf_op jit(solution)/shard_map/ppermute | solution.py:27
  49.9 12.8 %collective-permute-done.3 = f32[25,2,2,132]{3,2,1,0:T(2,128)S(1)} collective-permute-done((f32[25,2,2,132]{3,2,1,0:T(2,128)S(1)}, f32[25,2,2,132]{3,2,1,0:T(2,128)S(1)}, u32[]{:S(2)}, u32[]{:S(2)}) %collective-permute-start.3) | collective-permute-done | bytes 52832 | tf_op jit(solution)/shard_map/ppermute | solution.py:30
  65.8 3.6 %collective-permute-start.5 = (f32[25,2,20,132]{3,1,2,0:T(2,128)S(1)}, f32[25,2,20,132]{3,1,2,0:T(2,128)S(1)}, u32[]{:S(2)}, u32[]{:S(2)}) collective-permute-start(f32[25,2,20,132]{3,1,2,0:T(2,128)S(1)} %copy.9), channel_id=1, source_target_pairs={{1,0},{2,1},{3,2},{4,3},{5,4},{6,5},{7,6},{8,7},{9,8},{10,9},{11,1... | collective-permute-start | bytes 1584008 | tf_op jit(solution)/shard_map/ppermute | solution.py:30
  70.3 9.4 %collective-permute-done.4 = f32[25,2,20,132]{3,1,2,0:T(2,128)S(1)} collective-permute-done((f32[25,2,20,132]{3,1,2,0:T(2,128)S(1)}, f32[25,2,20,132]{3,1,2,0:T(2,128)S(1)}, u32[]{:S(2)}, u32[]{:S(2)}) %collective-permute-start.4) | collective-permute-done | bytes 528032 | tf_op jit(solution)/shard_map/ppermute | solution.py:27
  79.8 6.4 %collective-permute-done.5 = f32[25,2,20,132]{3,1,2,0:T(2,128)S(1)} collective-permute-done((f32[25,2,20,132]{3,1,2,0:T(2,128)S(1)}, f32[25,2,20,132]{3,1,2,0:T(2,128)S(1)}, u32[]{:S(2)}, u32[]{:S(2)}) %collective-permute-start.5) | collective-permute-done | bytes 528032 | tf_op jit(solution)/shard_map/ppermute | solution.py:30
  92.5 3.5 %collective-permute-start.7 = (f32[25,2,16,128]{3,2,1,0:T(8,128)S(1)}, f32[25,2,16,128]{3,2,1,0:T(8,128)S(1)}, u32[]{:S(2)}, u32[]{:S(2)}) collective-permute-start(f32[25,2,16,128]{3,2,1,0:T(8,128)S(1)} %multiply_add_fusion.1.refs_0_), channel_id=1, source_target_pairs={{0,256},{1,769},{2,258},{3,771},{4,260},{5,773},{6,262},{7,775},{8... | collective-permute-start | bytes 1228808 | tf_op jit(solution)/shard_map/ppermute | solution.py:350
  96.0 8.6 %collective-permute-start.6 = (f32[25,2,16,128]{3,2,1,0:T(8,128)S(1)}, f32[25,2,16,128]{3,2,1,0:T(8,128)S(1)}, u32[]{:S(2)}, u32[]{:S(2)}) collective-permute-start(f32[25,2,16,128]{3,2,1,0:T(8,128)S(1)} %multiply_add_fusion.1.refs_0_), channel_id=1, source_target_pairs={{0,64},{1,193},{2,66},{3,195},{4,68},{5,197},{6,70},{7,199},{8,72}... | collective-permute-start | bytes 1228808 | tf_op jit(solution)/shard_map/ppermute | solution.py:349
  104.6 3.6 %collective-permute-start.9 = (f32[25,2,16,128]{3,2,1,0:T(8,128)S(1)}, f32[25,2,16,128]{3,2,1,0:T(8,128)S(1)}, u32[]{:S(2)}, u32[]{:S(2)}) collective-permute-start(f32[25,2,16,128]{3,2,1,0:T(8,128)S(1)} %multiply_add_fusion.1.refs_0_), channel_id=1, source_target_pairs={{0,768},{1,257},{2,770},{3,259},{4,772},{5,261},{6,774},{7,263},{8... | collective-permute-start | bytes 1228808 | tf_op jit(solution)/shard_map/ppermute | solution.py:351
  110.5 21.4 %collective-permute-done.6.refs_0_ = f32[25,2,16,128]{3,2,1,0:T(8,128)S(1)} collective-permute-done((f32[25,2,16,128]{3,2,1,0:T(8,128)S(1)}, f32[25,2,16,128]{3,2,1,0:T(8,128)S(1)}, u32[]{:S(2)}, u32[]{:S(2)}) %collective-permute-start.6) | collective-permute-done | bytes 409632 | tf_op jit(solution)/shard_map/ppermute | solution.py:349
  135.1 63.1 %collective-permute-start.10 = (f32[25,2,16,128]{3,2,1,0:T(8,128)S(1)}, f32[25,2,16,128]{3,2,1,0:T(8,128)S(1)}, u32[]{:S(2)}, u32[]{:S(2)}) collective-permute-start(f32[25,2,16,128]{3,2,1,0:T(8,128)S(1)} %collective-permute-done.6.refs_0_), channel_id=1, source_target_pairs={{0,64},{1,193},{2,66},{3,195},{4,68},{5,197},{6,70},{7,199},{8,72}... | collective-permute-start | bytes 1228808 | tf_op jit(solution)/shard_map/ppermute | solution.py:349
  198.3 5.1 %collective-permute-start.13 = (f32[25,2,16,128]{3,2,1,0:T(8,128)S(1)}, f32[25,2,16,128]{3,2,1,0:T(8,128)S(1)}, u32[]{:S(2)}, u32[]{:S(2)}) collective-permute-start(f32[25,2,16,128]{3,2,1,0:T(8,128)S(1)} %collective-permute-done.6.refs_0_), channel_id=1, source_target_pairs={{0,768},{1,257},{2,770},{3,259},{4,772},{5,261},{6,774},{7,263},{8... | collective-permute-start | bytes 1228808 | tf_op jit(solution)/shard_map/ppermute | solution.py:351
  205.3 8.3 %collective-permute-done.10.refs_0_ = f32[25,2,16,128]{3,2,1,0:T(8,128)S(1)} collective-permute-done((f32[25,2,16,128]{3,2,1,0:T(8,128)S(1)}, f32[25,2,16,128]{3,2,1,0:T(8,128)S(1)}, u32[]{:S(2)}, u32[]{:S(2)}) %collective-permute-start.10) | collective-permute-done | bytes 409632 | tf_op jit(solution)/shard_map/ppermute | solution.py:349
  214.7 4.4 %collective-permute-start.15 = (f32[25,2,16,128]{3,2,1,0:T(8,128)S(1)}, f32[25,2,16,128]{3,2,1,0:T(8,128)S(1)}, u32[]{:S(2)}, u32[]{:S(2)}) collective-permute-start(f32[25,2,16,128]{3,2,1,0:T(8,128)S(1)} %collective-permute-done.10.refs_0_), channel_id=1, source_target_pairs={{0,256},{1,769},{2,258},{3,771},{4,260},{5,773},{6,262},{7,775},{8... | collective-permute-start | bytes 1228808 | tf_op jit(solution)/shard_map/ppermute | solution.py:350
  219.1 10.4 %collective-permute-start.14 = (f32[25,2,16,128]{3,2,1,0:T(8,128)S(1)}, f32[25,2,16,128]{3,2,1,0:T(8,128)S(1)}, u32[]{:S(2)}, u32[]{:S(2)}) collective-permute-start(f32[25,2,16,128]{3,2,1,0:T(8,128)S(1)} %collective-permute-done.10.refs_0_), channel_id=1, source_target_pairs={{0,64},{1,193},{2,66},{3,195},{4,68},{5,197},{6,70},{7,199},{8,72}... | collective-permute-start | bytes 1228808 | tf_op jit(solution)/shard_map/ppermute | solution.py:349
  229.5 5.1 %collective-permute-start.17 = (f32[25,2,16,128]{3,2,1,0:T(8,128)S(1)}, f32[25,2,16,128]{3,2,1,0:T(8,128)S(1)}, u32[]{:S(2)}, u32[]{:S(2)}) collective-permute-start(f32[25,2,16,128]{3,2,1,0:T(8,128)S(1)} %collective-permute-done.10.refs_0_), channel_id=1, source_target_pairs={{0,768},{1,257},{2,770},{3,259},{4,772},{5,261},{6,774},{7,263},{8... | collective-permute-start | bytes 1228808 | tf_op jit(solution)/shard_map/ppermute | solution.py:351
  240.1 5.6 %collective-permute-done.16.refs_2_ = f32[25,2,16,128]{3,2,1,0:T(8,128)S(1)} collective-permute-done((f32[25,2,16,128]{3,2,1,0:T(8,128)S(1)}, f32[25,2,16,128]{3,2,1,0:T(8,128)S(1)}, u32[]{:S(2)}, u32[]{:S(2)}) %collective-permute-start.16) | collective-permute-done | bytes 409632 | tf_op jit(solution)/shard_map/ppermute | solution.py:352
  247.6 5.1 %collective-permute-start.20 = (f32[25,2,16,128]{3,2,1,0:T(8,128)S(1)}, f32[25,2,16,128]{3,2,1,0:T(8,128)S(1)}, u32[]{:S(2)}, u32[]{:S(2)}) collective-permute-start(f32[25,2,16,128]{3,2,1,0:T(8,128)S(1)} %collective-permute-done.14.refs_0_), channel_id=1, source_target_pairs={{0,768},{1,257},{2,770},{3,259},{4,772},{5,261},{6,774},{7,263},{8... | collective-permute-start | bytes 1228808 | tf_op jit(solution)/shard_map/ppermute | solution.py:351
  252.7 8.0 %collective-permute-done.18.refs_1_ = f32[25,2,16,128]{3,2,1,0:T(8,128)S(1)} collective-permute-done((f32[25,2,16,128]{3,2,1,0:T(8,128)S(1)}, f32[25,2,16,128]{3,2,1,0:T(8,128)S(1)}, u32[]{:S(2)}, u32[]{:S(2)}) %collective-permute-start.18) | collective-permute-done | bytes 409632 | tf_op jit(solution)/shard_map/ppermute | solution.py:350
  266.4 5.4 %collective-permute-done.19.refs_2_ = f32[25,2,16,128]{3,2,1,0:T(8,128)S(1)} collective-permute-done((f32[25,2,16,128]{3,2,1,0:T(8,128)S(1)}, f32[25,2,16,128]{3,2,1,0:T(8,128)S(1)}, u32[]{:S(2)}, u32[]{:S(2)}) %collective-permute-start.19) | collective-permute-done | bytes 409632 | tf_op jit(solution)/shard_map/ppermute | solution.py:352
  (72 shorter events, 36.4 us)
Async XLA Ops:
  0.6 17.7 %copy-start.1 = (f32[25,2,16,128]{3,2,1,0:T(8,128)S(1)}, f32[25,2,16,128]{3,2,1,0:T(8,128)}, u32[]{:S(2)}) copy-start(f32[25,2,16,128]{3,2,1,0:T(8,128)} %param.3) | copy-start | bytes 1228804
  2.0 14.4 %collective-permute-start = (f32[25,2,16,2]{3,2,1,0:T(8,128)S(1)}, f32[25,2,16,2]{3,2,1,0:T(8,128)S(1)}, u32[]{:S(2)}, u32[]{:S(2)}) collective-permute-start(f32[25,2,16,2]{3,2,1,0:T(8,128)S(1)} %get-tuple-element.60), channel_id=1, source_target_pairs={{0,256},{256,512},{512,768},{768,0},{1,257},{257,513},{513,769},{7... | collective-permute-start | bytes 19208 | tf_op jit(solution)/shard_map/ppermute | solution.py:27
  5.5 12.8 %collective-permute-start.1 = (f32[25,2,16,2]{3,2,1,0:T(8,128)S(1)}, f32[25,2,16,2]{3,2,1,0:T(8,128)S(1)}, u32[]{:S(2)}, u32[]{:S(2)}) collective-permute-start(f32[25,2,16,2]{3,2,1,0:T(8,128)S(1)} %get-tuple-element.61), channel_id=1, source_target_pairs={{256,0},{512,256},{768,512},{0,768},{257,1},{513,257},{769,513},{1... | collective-permute-start | bytes 19208 | tf_op jit(solution)/shard_map/ppermute | solution.py:30
  18.7 31.2 %collective-permute-start.2 = (f32[25,2,2,132]{3,2,1,0:T(2,128)S(1)}, f32[25,2,2,132]{3,2,1,0:T(2,128)S(1)}, u32[]{:S(2)}, u32[]{:S(2)}) collective-permute-start(f32[25,2,2,132]{3,2,1,0:T(2,128)S(1)} %get-tuple-element.57), channel_id=1, source_target_pairs={{0,64},{64,128},{128,192},{192,0},{1,65},{65,129},{129,193},{193,1... | collective-permute-start | bytes 158408 | tf_op jit(solution)/shard_map/ppermute | solution.py:27
  34.5 28.3 %collective-permute-start.3 = (f32[25,2,2,132]{3,2,1,0:T(2,128)S(1)}, f32[25,2,2,132]{3,2,1,0:T(2,128)S(1)}, u32[]{:S(2)}, u32[]{:S(2)}) collective-permute-start(f32[25,2,2,132]{3,2,1,0:T(2,128)S(1)} %get-tuple-element.58), channel_id=1, source_target_pairs={{64,0},{128,64},{192,128},{0,192},{65,1},{129,65},{193,129},{1,193... | collective-permute-start | bytes 158408 | tf_op jit(solution)/shard_map/ppermute | solution.py:30
  63.8 15.9 %collective-permute-start.4 = (f32[25,2,20,132]{3,1,2,0:T(2,128)S(1)}, f32[25,2,20,132]{3,1,2,0:T(2,128)S(1)}, u32[]{:S(2)}, u32[]{:S(2)}) collective-permute-start(f32[25,2,20,132]{3,1,2,0:T(2,128)S(1)} %copy.9), channel_id=1, source_target_pairs={{0,1},{1,2},{2,3},{3,4},{4,5},{5,6},{6,7},{7,8},{8,9},{9,10},{10,1... | collective-permute-start | bytes 1584008 | tf_op jit(solution)/shard_map/ppermute | solution.py:27
  65.8 20.4 %collective-permute-start.5 = (f32[25,2,20,132]{3,1,2,0:T(2,128)S(1)}, f32[25,2,20,132]{3,1,2,0:T(2,128)S(1)}, u32[]{:S(2)}, u32[]{:S(2)}) collective-permute-start(f32[25,2,20,132]{3,1,2,0:T(2,128)S(1)} %copy.9), channel_id=1, source_target_pairs={{1,0},{2,1},{3,2},{4,3},{5,4},{6,5},{7,6},{8,7},{9,8},{10,9},{11,1... | collective-permute-start | bytes 1584008 | tf_op jit(solution)/shard_map/ppermute | solution.py:30
  90.8 1.6 copy-start.3
  92.5 171.4 %copy-start = (f32[25,2,16,128]{3,2,1,0:T(8,128)}, f32[25,2,16,128]{3,2,1,0:T(8,128)S(1)}, u32[]{:S(2)}) copy-start(f32[25,2,16,128]{3,2,1,0:T(8,128)S(1)} %multiply_add_fusion.1.refs_0_) | copy-start | bytes 1228804
  92.5 15.7 %collective-permute-start.7 = (f32[25,2,16,128]{3,2,1,0:T(8,128)S(1)}, f32[25,2,16,128]{3,2,1,0:T(8,128)S(1)}, u32[]{:S(2)}, u32[]{:S(2)}) collective-permute-start(f32[25,2,16,128]{3,2,1,0:T(8,128)S(1)} %multiply_add_fusion.1.refs_0_), channel_id=1, source_target_pairs={{0,256},{1,769},{2,258},{3,771},{4,260},{5,773},{6,262},{7,775},{8... | collective-permute-start | bytes 1228808 | tf_op jit(solution)/shard_map/ppermute | solution.py:350
  96.0 35.9 %collective-permute-start.6 = (f32[25,2,16,128]{3,2,1,0:T(8,128)S(1)}, f32[25,2,16,128]{3,2,1,0:T(8,128)S(1)}, u32[]{:S(2)}, u32[]{:S(2)}) collective-permute-start(f32[25,2,16,128]{3,2,1,0:T(8,128)S(1)} %multiply_add_fusion.1.refs_0_), channel_id=1, source_target_pairs={{0,64},{1,193},{2,66},{3,195},{4,68},{5,197},{6,70},{7,199},{8,72}... | collective-permute-start | bytes 1228808 | tf_op jit(solution)/shard_map/ppermute | solution.py:349
  104.6 27.3 %collective-permute-start.9 = (f32[25,2,16,128]{3,2,1,0:T(8,128)S(1)}, f32[25,2,16,128]{3,2,1,0:T(8,128)S(1)}, u32[]{:S(2)}, u32[]{:S(2)}) collective-permute-start(f32[25,2,16,128]{3,2,1,0:T(8,128)S(1)} %multiply_add_fusion.1.refs_0_), channel_id=1, source_target_pairs={{0,768},{1,257},{2,770},{3,259},{4,772},{5,261},{6,774},{7,263},{8... | collective-permute-start | bytes 1228808 | tf_op jit(solution)/shard_map/ppermute | solution.py:351
  108.2 23.7 %collective-permute-start.8 = (f32[25,2,16,128]{3,2,1,0:T(8,128)S(1)}, f32[25,2,16,128]{3,2,1,0:T(8,128)S(1)}, u32[]{:S(2)}, u32[]{:S(2)}) collective-permute-start(f32[25,2,16,128]{3,2,1,0:T(8,128)S(1)} %collective-permute-done.7.refs_1_), channel_id=1, source_target_pairs={{0,256},{1,769},{2,258},{3,771},{4,260},{5,773},{6,262},{7,775},{8... | collective-permute-start | bytes 1228808 | tf_op jit(solution)/shard_map/ppermute | solution.py:352
  131.9 71.5 %collective-permute-start.11 = (f32[25,2,16,128]{3,2,1,0:T(8,128)S(1)}, f32[25,2,16,128]{3,2,1,0:T(8,128)S(1)}, u32[]{:S(2)}, u32[]{:S(2)}) collective-permute-start(f32[25,2,16,128]{3,2,1,0:T(8,128)S(1)} %collective-permute-done.6.refs_0_), channel_id=1, source_target_pairs={{0,256},{1,769},{2,258},{3,771},{4,260},{5,773},{6,262},{7,775},{8... | collective-permute-start | bytes 1228808 | tf_op jit(solution)/shard_map/ppermute | solution.py:350
  135.1 78.5 %collective-permute-start.10 = (f32[25,2,16,128]{3,2,1,0:T(8,128)S(1)}, f32[25,2,16,128]{3,2,1,0:T(8,128)S(1)}, u32[]{:S(2)}, u32[]{:S(2)}) collective-permute-start(f32[25,2,16,128]{3,2,1,0:T(8,128)S(1)} %collective-permute-done.6.refs_0_), channel_id=1, source_target_pairs={{0,64},{1,193},{2,66},{3,195},{4,68},{5,197},{6,70},{7,199},{8,72}... | collective-permute-start | bytes 1228808 | tf_op jit(solution)/shard_map/ppermute | solution.py:349
  198.3 15.4 %collective-permute-start.13 = (f32[25,2,16,128]{3,2,1,0:T(8,128)S(1)}, f32[25,2,16,128]{3,2,1,0:T(8,128)S(1)}, u32[]{:S(2)}, u32[]{:S(2)}) collective-permute-start(f32[25,2,16,128]{3,2,1,0:T(8,128)S(1)} %collective-permute-done.6.refs_0_), channel_id=1, source_target_pairs={{0,768},{1,257},{2,770},{3,259},{4,772},{5,261},{6,774},{7,263},{8... | collective-permute-start | bytes 1228808 | tf_op jit(solution)/shard_map/ppermute | solution.py:351
  203.4 11.3 %collective-permute-start.12 = (f32[25,2,16,128]{3,2,1,0:T(8,128)S(1)}, f32[25,2,16,128]{3,2,1,0:T(8,128)S(1)}, u32[]{:S(2)}, u32[]{:S(2)}) collective-permute-start(f32[25,2,16,128]{3,2,1,0:T(8,128)S(1)} %collective-permute-done.11.refs_1_), channel_id=1, source_target_pairs={{0,256},{1,769},{2,258},{3,771},{4,260},{5,773},{6,262},{7,775},{8... | collective-permute-start | bytes 1228808 | tf_op jit(solution)/shard_map/ppermute | solution.py:352
  214.7 19.9 %collective-permute-start.15 = (f32[25,2,16,128]{3,2,1,0:T(8,128)S(1)}, f32[25,2,16,128]{3,2,1,0:T(8,128)S(1)}, u32[]{:S(2)}, u32[]{:S(2)}) collective-permute-start(f32[25,2,16,128]{3,2,1,0:T(8,128)S(1)} %collective-permute-done.10.refs_0_), channel_id=1, source_target_pairs={{0,256},{1,769},{2,258},{3,771},{4,260},{5,773},{6,262},{7,775},{8... | collective-permute-start | bytes 1228808 | tf_op jit(solution)/shard_map/ppermute | solution.py:350
  219.1 19.8 %collective-permute-start.14 = (f32[25,2,16,128]{3,2,1,0:T(8,128)S(1)}, f32[25,2,16,128]{3,2,1,0:T(8,128)S(1)}, u32[]{:S(2)}, u32[]{:S(2)}) collective-permute-start(f32[25,2,16,128]{3,2,1,0:T(8,128)S(1)} %collective-permute-done.10.refs_0_), channel_id=1, source_target_pairs={{0,64},{1,193},{2,66},{3,195},{4,68},{5,197},{6,70},{7,199},{8,72}... | collective-permute-start | bytes 1228808 | tf_op jit(solution)/shard_map/ppermute | solution.py:349
  229.5 10.6 %collective-permute-start.17 = (f32[25,2,16,128]{3,2,1,0:T(8,128)S(1)}, f32[25,2,16,128]{3,2,1,0:T(8,128)S(1)}, u32[]{:S(2)}, u32[]{:S(2)}) collective-permute-start(f32[25,2,16,128]{3,2,1,0:T(8,128)S(1)} %collective-permute-done.10.refs_0_), channel_id=1, source_target_pairs={{0,768},{1,257},{2,770},{3,259},{4,772},{5,261},{6,774},{7,263},{8... | collective-permute-start | bytes 1228808 | tf_op jit(solution)/shard_map/ppermute | solution.py:351
  234.6 11.1 %collective-permute-start.16 = (f32[25,2,16,128]{3,2,1,0:T(8,128)S(1)}, f32[25,2,16,128]{3,2,1,0:T(8,128)S(1)}, u32[]{:S(2)}, u32[]{:S(2)}) collective-permute-start(f32[25,2,16,128]{3,2,1,0:T(8,128)S(1)} %collective-permute-done.15.refs_1_), channel_id=1, source_target_pairs={{0,256},{1,769},{2,258},{3,771},{4,260},{5,773},{6,262},{7,775},{8... | collective-permute-start | bytes 1228808 | tf_op jit(solution)/shard_map/ppermute | solution.py:352
  245.7 15.1 %collective-permute-start.18 = (f32[25,2,16,128]{3,2,1,0:T(8,128)S(1)}, f32[25,2,16,128]{3,2,1,0:T(8,128)S(1)}, u32[]{:S(2)}, u32[]{:S(2)}) collective-permute-start(f32[25,2,16,128]{3,2,1,0:T(8,128)S(1)} %collective-permute-done.14.refs_0_), channel_id=1, source_target_pairs={{0,256},{1,769},{2,258},{3,771},{4,260},{5,773},{6,262},{7,775},{8... | collective-permute-start | bytes 1228808 | tf_op jit(solution)/shard_map/ppermute | solution.py:350
  247.6 18.8 %collective-permute-start.20 = (f32[25,2,16,128]{3,2,1,0:T(8,128)S(1)}, f32[25,2,16,128]{3,2,1,0:T(8,128)S(1)}, u32[]{:S(2)}, u32[]{:S(2)}) collective-permute-start(f32[25,2,16,128]{3,2,1,0:T(8,128)S(1)} %collective-permute-done.14.refs_0_), channel_id=1, source_target_pairs={{0,768},{1,257},{2,770},{3,259},{4,772},{5,261},{6,774},{7,263},{8... | collective-permute-start | bytes 1228808 | tf_op jit(solution)/shard_map/ppermute | solution.py:351
  260.8 11.0 %collective-permute-start.19 = (f32[25,2,16,128]{3,2,1,0:T(8,128)S(1)}, f32[25,2,16,128]{3,2,1,0:T(8,128)S(1)}, u32[]{:S(2)}, u32[]{:S(2)}) collective-permute-start(f32[25,2,16,128]{3,2,1,0:T(8,128)S(1)} %collective-permute-done.18.refs_1_), channel_id=1, source_target_pairs={{0,256},{1,769},{2,258},{3,771},{4,260},{5,773},{6,262},{7,775},{8... | collective-permute-start | bytes 1228808 | tf_op jit(solution)/shard_map/ppermute | solution.py:352
  (1 other events, 1.0 us)

commit v2 on v1

--- a/solution.py
+++ b/solution.py
@@ -7,87 +7,237 @@
 
 
 STEP_DT = 0.25
-SPACING = 1.0
 DISSIPATE = 0.1
 DRIVER_ETA = 2.0
 KAPPA_ONE = 0.1
-FIRST_TAPS = (1.0 / 12.0, -8.0 / 12.0, 0.0, 8.0 / 12.0, -1.0 / 12.0)
-SECOND_TAPS = (-1.0 / 12.0, 16.0 / 12.0, -30.0 / 12.0, 16.0 / 12.0, -1.0 / 12.0)
-FOURTH_TAPS = (1.0, -4.0, 6.0, -4.0, 1.0)
 PAIR_SLOT = ((0, 1, 2), (1, 3, 4), (2, 4, 5))
 PAIR_LIST = ((0, 0), (0, 1), (0, 2), (1, 1), (1, 2), (2, 2))
 
 
-def extended(block, sides, width):
-    for axis, dim in sides:
-        count = lax.axis_size(axis)
-        forward = [(i, i + 1) for i in range(count - 1)]
-        forward.append((count - 1, 0))
-        backward = [(target, source) for source, target in forward]
-        low = lax.ppermute(
-            lax.slice_in_dim(block, block.shape[dim] - width, None, axis=dim), axis, forward
-        )
-        high = lax.ppermute(lax.slice_in_dim(block, 0, width, axis=dim), axis, backward)
-        block = jnp.concatenate([low, block, high], axis=dim)
-    return block
-
-
-def window(padded, shifts):
-    interior = (padded.shape[1] - 4, padded.shape[2] - 4, padded.shape[3] - 4)
-    corner = (2 + shifts[2], 2 + shifts[1], 2 + shifts[0])
-    return padded[
-        :,
-        corner[0] : corner[0] + interior[0],
-        corner[1] : corner[1] + interior[1],
-        corner[2] : corner[2] + interior[2],
-    ]
-
-
-def moved(direction, amount):
-    shifts = [0, 0, 0]
-    shifts[direction] = amount
-    return shifts
-
-
-def line_sum(padded, direction, weights):
-    running = None
-    for position in range(5):
-        if weights[position] != 0.0:
-            weighted = weights[position] * window(padded, moved(direction, position - 2))
-            running = weighted if running is None else running + weighted
-    return running
-
-
-def cross_sum(padded, first_dir, second_dir):
-    running = None
-    for first_pos in range(5):
-        for second_pos in range(5):
-            factor = FIRST_TAPS[first_pos] * FIRST_TAPS[second_pos]
-            if factor != 0.0:
-                shifts = [0, 0, 0]
-                shifts[first_dir] = first_pos - 2
-                shifts[second_dir] = second_pos - 2
-                weighted = factor * window(padded, shifts)
-                running = weighted if running is None else running + weighted
-    return running
-
-
-def evolve_rate(padded):
-    centre = window(padded, (0, 0, 0))
-    gradients = [line_sum(padded, direction, FIRST_TAPS) / SPACING for direction in range(3)]
-    curves = [
-        line_sum(padded, direction, SECOND_TAPS) / (SPACING * SPACING) for direction in range(3)
-    ]
-    smoothing = (
-        line_sum(padded, 0, FOURTH_TAPS)
-        + line_sum(padded, 1, FOURTH_TAPS)
-        + line_sum(padded, 2, FOURTH_TAPS)
-    )
-    chosen = jnp.concatenate([padded[0:1], padded[17:21]], axis=0)
-    mixed_terms = {}
-    for dir_pair in ((0, 1), (0, 2), (1, 2)):
-        mixed_terms[dir_pair] = cross_sum(chosen, dir_pair[0], dir_pair[1]) / (SPACING * SPACING)
-
+EDGED = (0, 17, 18, 19, 20)
+PAD = 8
+
+
+def rolled(tile, amount):
+    amount = amount % 128
+    return tile if amount == 0 else pltpu.roll(tile, amount, 1)
+
+
+def lanes_of(tile):
+    return lax.broadcasted_iota(jnp.int32, tile.shape, 1)
+
+
+def pack_kernel(section, left, right, top, bottom):
+    fields_count, planes, rows, cols = section.shape
+    low = jnp.zeros((rows, cols), jnp.float32)
+    high = jnp.zeros((rows, cols), jnp.float32)
+    lane_pair = lanes_of(low) // 2
+    for field in range(fields_count):
+        for plane in range(planes):
+            number = field * planes + plane
+            tile = section[field, plane]
+            low = jnp.where(lane_pair == number, rolled(tile, 2 * number), low)
+            high = jnp.where(lane_pair == number, rolled(tile, 2 * number + 2), high)
+            top[2 * number : 2 * number + 2, :] = section[field, plane, 0:2, :]
+            bottom[2 * number : 2 * number + 2, :] = section[field, plane, rows - 2 : rows, :]
+    left[...] = low
+    right[...] = high
+
+
+def edge_kernel(from_left, from_right, from_low, from_high, edges, left, right):
+    edges[0:16, :] = from_left[...]
+    edges[16:32, :] = from_right[...]
+    for side, rows in enumerate((from_low, from_high)):
+        low = jnp.zeros((2, 128), jnp.float32)
+        high = jnp.zeros((2, 128), jnp.float32)
+        lane_pair = lanes_of(low) // 2
+        for slot, field in enumerate(EDGED):
+            for plane in range(2):
+                number = slot * 2 + plane
+                tile = rows[4 * field + 2 * plane : 4 * field + 2 * plane + 2, :]
+                place = 32 + 20 * side + 2 * number
+                edges[place : place + 2, :] = tile
+                low = jnp.where(lane_pair == number, rolled(tile, 2 * number), low)
+                high = jnp.where(lane_pair == number, rolled(tile, 2 * number + 2), high)
+        left[2 * side : 2 * side + 2, :] = low
+        right[2 * side : 2 * side + 2, :] = high
+
+
+def border(from_left, from_right, number):
+    return jnp.where(
+        lanes_of(from_left) >= 64,
+        rolled(from_left, 126 - 2 * number),
+        rolled(from_right, 128 - 2 * number),
+    )
+
+
+def along_lanes(tile, edge):
+    lane = lanes_of(tile)
+    return (
+        rolled(jnp.where(lane >= 126, edge, tile), 2),
+        rolled(jnp.where(lane == 127, edge, tile), 1),
+        rolled(jnp.where(lane == 0, edge, tile), 127),
+        rolled(jnp.where(lane <= 1, edge, tile), 126),
+    )
+
+
+def slope(around):
+    back2, back1, ahead1, ahead2 = around
+    return (8.0 / 12.0) * (ahead1 - back1) - (1.0 / 12.0) * (ahead2 - back2)
+
+
+def rate_kernel(
+    section,
+    below,
+    above,
+    from_left,
+    from_right,
+    from_low,
+    from_high,
+    edges_below,
+    edges_above,
+    corner_left,
+    corner_right,
+    base,
+    accum,
+    next_section,
+    next_accum,
+    ext,
+    cross_x,
+    cross_y,
+):
+    fields_count, planes, rows, _ = section.shape
+    last = PAD + rows
+    for field in range(fields_count):
+        for plane in range(planes):
+            number = 2 * (field * planes + plane)
+            ext[field, plane, PAD:last, :] = section[field, plane]
+            ext[field, plane, PAD - 2 : PAD, :] = from_low[number : number + 2, :]
+            ext[field, plane, last : last + 2, :] = from_high[number : number + 2, :]
+
+    def layer(field, plane):
+        if plane < 0:
+            return below[field, plane + 2]
+        if plane > 1:
+            return above[field, plane - 2]
+        return section[field, plane]
+
+    for slot, field in enumerate(EDGED):
+        for plane in range(-2, 4):
+            tile = layer(field, plane)
+            if plane in (0, 1):
+                edge = border(from_left[...], from_right[...], 2 * field + plane)
+                cross_x[slot, plane + 2, PAD:last, :] = slope(along_lanes(tile, edge))
+                for side, place in enumerate((PAD - 2, last)):
+                    strip = ext[field, plane, place : place + 2, :]
+                    edge = border(
+                        corner_left[2 * side : 2 * side + 2, :],
+                        corner_right[2 * side : 2 * side + 2, :],
+                        2 * slot + plane,
+                    )
+                    cross_x[slot, plane + 2, place : place + 2, :] = slope(
+                        along_lanes(strip, edge)
+                    )
+                column = ext.at[field, plane]
+            else:
+                source, local = (edges_below, plane + 2) if plane < 0 else (edges_above, plane - 2)
+                edge = border(source[0:16, :], source[16:32, :], 2 * field + local)
+                cross_x[slot, plane + 2, PAD:last, :] = slope(along_lanes(tile, edge))
+                place = 4 * slot + 2 * local
+                depth = fields_count + (plane + 2 if plane < 0 else plane)
+                column = ext.at[depth, slot % 2]
+                column[PAD:last, :] = tile
+                column[PAD - 2 : PAD, :] = source[32 + place : 34 + place, :]
+                column[last : last + 2, :] = source[52 + place : 54 + place, :]
+            cross_y[slot, plane + 2] = slope(
+                tuple(column[PAD + off : last + off, :] for off in (-2, -1, 1, 2))
+            )
+
+    for plane in range(planes):
+        write_rates(
+            plane,
+            section,
+            layer,
+            from_left,
+            from_right,
+            base,
+            accum,
+            next_section,
+            next_accum,
+            ext,
+            cross_x,
+            cross_y,
+        )
+
+
+def write_rates(
+    plane,
+    section,
+    layer,
+    from_left,
+    from_right,
+    base,
+    accum,
+    next_section,
+    next_accum,
+    ext,
+    cross_x,
+    cross_y,
+):
+    rows = section.shape[2]
+    last = PAD + rows
+    centre = [section[field, plane] for field in range(25)]
+    gradients = [[None] * 25 for _ in range(3)]
+    curves = [[None] * 25 for _ in range(3)]
+    smoothing = [None] * 25
+    for field in range(25):
+        tile = centre[field]
+        edge = border(from_left[...], from_right[...], 2 * field + plane)
+        around_x = along_lanes(tile, edge)
+        around_y = tuple(
+            ext[field, plane, PAD + off : last + off, :] for off in (-2, -1, 1, 2)
+        )
+        around_z = tuple(layer(field, plane + off) for off in (-2, -1, 1, 2))
+        total_near, total_far = None, None
+        for direction, around in enumerate((around_x, around_y, around_z)):
+            back2, back1, ahead1, ahead2 = around
+            near, far = back1 + ahead1, back2 + ahead2
+            gradients[direction][field] = slope(around)
+            if field <= 6 or 17 <= field <= 20:
+                curves[direction][field] = (
+                    (16.0 / 12.0) * near - (1.0 / 12.0) * far - (30.0 / 12.0) * tile
+                )
+            total_near = near if total_near is None else total_near + near
+            total_far = far if total_far is None else total_far + far
+        smoothing[field] = total_far - 4.0 * total_near + 18.0 * tile
+    mixed_terms = {(0, 1): [], (0, 2): [], (1, 2): []}
+    for slot in range(5):
+        mixed_terms[0, 1].append(
+            slope(
+                tuple(
+                    cross_x[slot, plane + 2, PAD + off : last + off, :]
+                    for off in (-2, -1, 1, 2)
+                )
+            )
+        )
+        mixed_terms[0, 2].append(
+            slope(
+                tuple(
+                    cross_x[slot, plane + 2 + off, PAD:last, :] for off in (-2, -1, 1, 2)
+                )
+            )
+        )
+        mixed_terms[1, 2].append(
+            slope(tuple(cross_y[slot, plane + 2 + off] for off in (-2, -1, 1, 2)))
+        )
+    rates = evolve_rate(centre, gradients, curves, mixed_terms)
+    for field in range(25):
+        rate = rates[field] + (-DISSIPATE / 16.0) * smoothing[field]
+        next_section[field, plane] = base[field, plane] + (0.5 * STEP_DT) * rate
+        next_accum[field, plane] = accum[field, plane] + (STEP_DT / 3.0) * rate
+
+
+def evolve_rate(centre, gradients, curves, mixed_terms):
     def second_of(chosen_slot, field_slot, axis_one, axis_two):
         if axis_one == axis_two:
             return curves[axis_one][field_slot]
@@ -266,7 +416,7 @@
         + 0.5 * lapse_field * (ricci_scalar + 2.0 / 3.0 * trace_curv * trace_curv - squares_a)
         - 2.0 * KAPPA_ONE * lapse_field * theta_field
     )
-    return jnp.stack(rates, axis=0) + -DISSIPATE / 16.0 * smoothing
+    return rates
 
 
 AXES = ("gx", "gy", "gz")
@@ -359,11 +509,80 @@
     return slab
 
 
+def ring(axis, step):
+    count = lax.axis_size(axis)
+    return [(source, (source + step) % count) for source in range(count)]
+
+
+def sent(array, axis, step):
+    return lax.ppermute(array, axis, ring(axis, step))
+
+
+def vmem(count):
+    return [pl.BlockSpec(memory_space=pltpu.VMEM)] * count
+
+
 def shards(section, base, accum):
-    padded = extended(section, (("gx", 3), ("gy", 2), ("gz", 1)), 2)
-    rates = evolve_rate(padded)
-    next_section = base + 0.5 * STEP_DT * rates
-    next_accum = accum + STEP_DT / 3.0 * rates
+    flat = jax.ShapeDtypeStruct((16, 128), jnp.float32)
+    strip = jax.ShapeDtypeStruct((100, 128), jnp.float32)
+    small = jax.ShapeDtypeStruct((4, 128), jnp.float32)
+    block = jax.ShapeDtypeStruct(section.shape, jnp.float32)
+    below = sent(section, "gz", 1)
+    above = sent(section, "gz", -1)
+    left, right, top, bottom = pl.pallas_call(
+        pack_kernel,
+        out_shape=(flat, flat, strip, strip),
+        in_specs=vmem(1),
+        out_specs=tuple(vmem(4)),
+        compiler_params=pltpu.CompilerParams(vmem_limit_bytes=4 * 1024 * 1024),
+        cost_estimate=pl.CostEstimate(flops=2000000, bytes_accessed=600000, transcendentals=0),
+        name="pack",
+    )(section)
+    from_low = sent(bottom, "gy", 1)
+    from_high = sent(top, "gy", -1)
+    from_left = sent(right, "gx", 1)
+    from_right = sent(left, "gx", -1)
+    edges, left, right = pl.pallas_call(
+        edge_kernel,
+        out_shape=(jax.ShapeDtypeStruct((72, 128), jnp.float32), small, small),
+        in_specs=vmem(4),
+        out_specs=tuple(vmem(3)),
+        compiler_params=pltpu.CompilerParams(vmem_limit_bytes=2 * 1024 * 1024),
+        cost_estimate=pl.CostEstimate(flops=200000, bytes_accessed=200000, transcendentals=0),
+        name="edge",
+    )(from_left, from_right, from_low, from_high)
+    edges_below = sent(edges, "gz", 1)
+    edges_above = sent(edges, "gz", -1)
+    corner_left = sent(right, "gx", 1)
+    corner_right = sent(left, "gx", -1)
+    next_section, next_accum = pl.pallas_call(
+        rate_kernel,
+        out_shape=(block, block),
+        in_specs=vmem(13),
+        out_specs=tuple(vmem(2)),
+        scratch_shapes=[
+            pltpu.VMEM((29, 2, 32, 128), jnp.float32),
+            pltpu.VMEM((5, 6, 32, 128), jnp.float32),
+            pltpu.VMEM((5, 6, 16, 128), jnp.float32),
+        ],
+        compiler_params=pltpu.CompilerParams(vmem_limit_bytes=16 * 1024 * 1024),
+        cost_estimate=pl.CostEstimate(flops=30000000, bytes_accessed=3000000, transcendentals=0),
+        name="rate",
+    )(
+        section,
+        below,
+        above,
+        from_left,
+        from_right,
+        from_low,
+        from_high,
+        edges_below,
+        edges_above,
+        corner_left,
+        corner_right,
+        base,
+        accum,
+    )
     return (next_section, next_accum, slab_of(next_section))
 
 

time: 274 us -> 235 us (0.86)
  the two profiles are of different devices: /device:TPU:66 before, /device:TPU:38 now
where the time goes in v2:
time: 235 us; the launch traced here: 234 us
  starting transfers between devices  124 us (53%)
  waiting for transfers between devices  90.6 us (39%)
  Pallas kernels  13.3 us (6%)
  local copies, waits for them, and re-layouts  5 us (2%)
    ppermute x3, waiting for transfers between devices, slab_of(): following = lax.ppermute(current, AXES, along_y)  71.1 us
    ppermute x10, starting transfers between devices, sent(): return lax.ppermute(array, axis, ring(axis, step))  48.3 us
    ppermute x3, starting transfers between devices, slab_of(): following = lax.ppermute(current, AXES, along_y)  35 us
    ppermute x4, starting transfers between devices, slab_of(): back = lax.ppermute(current, AXES, against_x)  17.7 us
    ppermute x4, starting transfers between devices, slab_of(): second = lax.ppermute(first, AXES, along_x)  11.5 us
    ppermute x4, starting transfers between devices, slab_of(): first = lax.ppermute(current, AXES, along_x)  11.4 us
    ppermute x10, waiting for transfers between devices, sent(): return lax.ppermute(array, axis, ring(axis, step))  11.3 us
    pallas_call x1, Pallas kernels, shards(): pl.pallas_call(rate_kernel, out_shape=(block, block), in_specs=vmem(13),...  8.15 us
  transfers between devices with their start and end apart: 25, of which 9 were waited for; matrix products, arithmetic and copies ran while one was open for 0% of the time, Pallas kernels for 2%

profile of v2, /device:TPU:38, one launch (start us, length us, event | category | flops | bytes accessed | tf_op | source)
XLA Modules:
  0.0 233.7 jit_solution(8445399298309916104)
XLA Ops:
  2.6 3.6 %collective-permute-start.1 = (f32[25,2,16,128]{3,2,1,0:T(8,128)}, f32[25,2,16,128]{3,2,1,0:T(8,128)S(1)}, u32[]{:S(2)}, u32[]{:S(2)}) collective-permute-start(f32[25,2,16,128]{3,2,1,0:T(8,128)} %section.3), channel_id=1, source_target_pairs={{0,63},{1,0},{2,1},{3,2},{4,3},{5,4},{6,5},{7,6},{8,7},{9,8},{10,9... | collective-permute-start | bytes 1228808 | tf_op jit(solution)/shard_map/ppermute | solution.py:518
  7.5 15.7 %collective-permute-start.4 = (f32[100,128]{1,0:T(8,128)S(1)}, f32[100,128]{1,0:T(8,128)S(1)}, u32[]{:S(2)}, u32[]{:S(2)}) collective-permute-start(f32[100,128]{1,0:T(8,128)S(1)} %get-tuple-element.26), channel_id=1, source_target_pairs={{0,64},{64,128},{128,192},{192,0},{1,65},{65,129},{129,193},{193,1... | collective-permute-start | bytes 153608 | tf_op jit(solution)/shard_map/ppermute | solution.py:518
  23.2 8.3 %collective-permute-start.5 = (f32[100,128]{1,0:T(8,128)S(1)}, f32[100,128]{1,0:T(8,128)S(1)}, u32[]{:S(2)}, u32[]{:S(2)}) collective-permute-start(f32[100,128]{1,0:T(8,128)S(1)} %get-tuple-element.27), channel_id=1, source_target_pairs={{0,192},{64,0},{128,64},{192,128},{1,193},{65,1},{129,65},{193,129... | collective-permute-start | bytes 153608 | tf_op jit(solution)/shard_map/ppermute | solution.py:518
  31.5 3.5 %collective-permute-start.2 = (f32[16,128]{1,0:T(8,128)S(1)}, f32[16,128]{1,0:T(8,128)S(1)}, u32[]{:S(2)}, u32[]{:S(2)}) collective-permute-start(f32[16,128]{1,0:T(8,128)S(1)} %get-tuple-element.24), channel_id=1, source_target_pairs={{0,256},{256,512},{512,768},{768,0},{1,257},{257,513},{513,769},{7... | collective-permute-start | bytes 24584 | tf_op jit(solution)/shard_map/ppermute | solution.py:518
  35.0 3.3 %collective-permute-done.2.from_left = f32[16,128]{1,0:T(8,128)S(1)} collective-permute-done((f32[16,128]{1,0:T(8,128)S(1)}, f32[16,128]{1,0:T(8,128)S(1)}, u32[]{:S(2)}, u32[]{:S(2)}) %collective-permute-start.2) | collective-permute-done | bytes 8224 | tf_op jit(solution)/shard_map/ppermute | solution.py:518
  38.3 3.7 %collective-permute-start.3 = (f32[16,128]{1,0:T(8,128)S(1)}, f32[16,128]{1,0:T(8,128)S(1)}, u32[]{:S(2)}, u32[]{:S(2)}) collective-permute-start(f32[16,128]{1,0:T(8,128)S(1)} %get-tuple-element.25), channel_id=1, source_target_pairs={{0,768},{256,0},{512,256},{768,512},{1,769},{257,1},{513,257},{769... | collective-permute-start | bytes 24584 | tf_op jit(solution)/shard_map/ppermute | solution.py:518
  45.9 3.6 %collective-permute-start.7 = (f32[72,128]{1,0:T(8,128)S(1)}, f32[72,128]{1,0:T(8,128)S(1)}, u32[]{:S(2)}, u32[]{:S(2)}) collective-permute-start(f32[72,128]{1,0:T(8,128)S(1)} %get-tuple-element.28), channel_id=1, source_target_pairs={{0,63},{1,0},{2,1},{3,2},{4,3},{5,4},{6,5},{7,6},{8,7},{9,8},{10,9... | collective-permute-start | bytes 110600 | tf_op jit(solution)/shard_map/ppermute | solution.py:518
  51.8 4.4 %collective-permute-done.8.corner_left = f32[4,128]{1,0:T(4,128)S(1)} collective-permute-done((f32[4,128]{1,0:T(4,128)S(1)}, f32[4,128]{1,0:T(4,128)S(1)}, u32[]{:S(2)}, u32[]{:S(2)}) %collective-permute-start.8) | collective-permute-done | bytes 2080 | tf_op jit(solution)/shard_map/ppermute | solution.py:518
  56.2 3.7 %collective-permute-start.9 = (f32[4,128]{1,0:T(4,128)S(1)}, f32[4,128]{1,0:T(4,128)S(1)}, u32[]{:S(2)}, u32[]{:S(2)}) collective-permute-start(f32[4,128]{1,0:T(4,128)S(1)} %get-tuple-element.30), channel_id=1, source_target_pairs={{0,768},{256,0},{512,256},{768,512},{1,769},{257,1},{513,257},{769... | collective-permute-start | bytes 6152 | tf_op jit(solution)/shard_map/ppermute | solution.py:518
  64.7 8.2 %rate.1 = (f32[25,2,16,128]{3,2,1,0:T(8,128)}, f32[25,2,16,128]{3,2,1,0:T(8,128)}) custom-call(f32[25,2,16,128]{3,2,1,0:T(8,128)S(1)} %copy-done.1, f32[25,2,16,128]{3,2,1,0:T(8,128)S(1)} %collective-permute-done.below, f32[25,2,16,128]{3,2,1,0:T(8,128)S(1)} %collective-permute-done.1.above, f32[16,128]{1,0:T(8,128)S(1)} %collective-permute-done.2.from_left, ...), custom_call_target="tpu_custom_call" | custom-call | flops 30000000 | bytes 3000000 | tf_op jit(solution)/shard_map/rate/pallas_call | solution.py:558
  74.8 14.4 %collective-permute-start.10 = (f32[25,2,16,128]{3,2,1,0:T(8,128)}, f32[25,2,16,128]{3,2,1,0:T(8,128)S(1)}, u32[]{:S(2)}, u32[]{:S(2)}) collective-permute-start(f32[25,2,16,128]{3,2,1,0:T(8,128)} %get-tuple-element.21.refs_0_), channel_id=1, source_target_pairs={{0,64},{1,193},{2,66},{3,195},{4,68},{5,197},{6,70},{7,199},{8,72}... | collective-permute-start | bytes 1228808 | tf_op jit(solution)/shard_map/ppermute | solution.py:499
  89.2 4.8 %collective-permute-start.13 = (f32[25,2,16,128]{3,2,1,0:T(8,128)}, f32[25,2,16,128]{3,2,1,0:T(8,128)S(1)}, u32[]{:S(2)}, u32[]{:S(2)}) collective-permute-start(f32[25,2,16,128]{3,2,1,0:T(8,128)} %get-tuple-element.21.refs_0_), channel_id=1, source_target_pairs={{0,768},{1,257},{2,770},{3,259},{4,772},{5,261},{6,774},{7,263},{8... | collective-permute-start | bytes 1228808 | tf_op jit(solution)/shard_map/ppermute | solution.py:501
  95.9 27.4 %collective-permute-done.10.refs_0_ = f32[25,2,16,128]{3,2,1,0:T(8,128)S(1)} collective-permute-done((f32[25,2,16,128]{3,2,1,0:T(8,128)}, f32[25,2,16,128]{3,2,1,0:T(8,128)S(1)}, u32[]{:S(2)}, u32[]{:S(2)}) %collective-permute-start.10) | collective-permute-done | bytes 409632 | tf_op jit(solution)/shard_map/ppermute | solution.py:499
  126.4 13.1 %collective-permute-start.14 = (f32[25,2,16,128]{3,2,1,0:T(8,128)S(1)}, f32[25,2,16,128]{3,2,1,0:T(8,128)S(1)}, u32[]{:S(2)}, u32[]{:S(2)}) collective-permute-start(f32[25,2,16,128]{3,2,1,0:T(8,128)S(1)} %collective-permute-done.10.refs_0_), channel_id=1, source_target_pairs={{0,64},{1,193},{2,66},{3,195},{4,68},{5,197},{6,70},{7,199},{8,72}... | collective-permute-start | bytes 1228808 | tf_op jit(solution)/shard_map/ppermute | solution.py:499
  139.4 4.8 %collective-permute-start.17 = (f32[25,2,16,128]{3,2,1,0:T(8,128)S(1)}, f32[25,2,16,128]{3,2,1,0:T(8,128)S(1)}, u32[]{:S(2)}, u32[]{:S(2)}) collective-permute-start(f32[25,2,16,128]{3,2,1,0:T(8,128)S(1)} %collective-permute-done.10.refs_0_), channel_id=1, source_target_pairs={{0,768},{1,257},{2,770},{3,259},{4,772},{5,261},{6,774},{7,263},{8... | collective-permute-start | bytes 1228808 | tf_op jit(solution)/shard_map/ppermute | solution.py:501
  147.5 21.8 %collective-permute-done.14.refs_0_ = f32[25,2,16,128]{3,2,1,0:T(8,128)S(1)} collective-permute-done((f32[25,2,16,128]{3,2,1,0:T(8,128)S(1)}, f32[25,2,16,128]{3,2,1,0:T(8,128)S(1)}, u32[]{:S(2)}, u32[]{:S(2)}) %collective-permute-start.14) | collective-permute-done | bytes 409632 | tf_op jit(solution)/shard_map/ppermute | solution.py:499
  172.4 7.5 %collective-permute-start.18 = (f32[25,2,16,128]{3,2,1,0:T(8,128)S(1)}, f32[25,2,16,128]{3,2,1,0:T(8,128)S(1)}, u32[]{:S(2)}, u32[]{:S(2)}) collective-permute-start(f32[25,2,16,128]{3,2,1,0:T(8,128)S(1)} %collective-permute-done.14.refs_0_), channel_id=1, source_target_pairs={{0,64},{1,193},{2,66},{3,195},{4,68},{5,197},{6,70},{7,199},{8,72}... | collective-permute-start | bytes 1228808 | tf_op jit(solution)/shard_map/ppermute | solution.py:499
  179.9 4.4 %collective-permute-start.21 = (f32[25,2,16,128]{3,2,1,0:T(8,128)S(1)}, f32[25,2,16,128]{3,2,1,0:T(8,128)S(1)}, u32[]{:S(2)}, u32[]{:S(2)}) collective-permute-start(f32[25,2,16,128]{3,2,1,0:T(8,128)S(1)} %collective-permute-done.14.refs_0_), channel_id=1, source_target_pairs={{0,768},{1,257},{2,770},{3,259},{4,772},{5,261},{6,774},{7,263},{8... | collective-permute-start | bytes 1228808 | tf_op jit(solution)/shard_map/ppermute | solution.py:501
  184.4 4.2 %collective-permute-start.20 = (f32[25,2,16,128]{3,2,1,0:T(8,128)S(1)}, f32[25,2,16,128]{3,2,1,0:T(8,128)S(1)}, u32[]{:S(2)}, u32[]{:S(2)}) collective-permute-start(f32[25,2,16,128]{3,2,1,0:T(8,128)S(1)} %collective-permute-done.19.refs_1_), channel_id=1, source_target_pairs={{0,256},{1,769},{2,258},{3,771},{4,260},{5,773},{6,262},{7,775},{8... | collective-permute-start | bytes 1228808 | tf_op jit(solution)/shard_map/ppermute | solution.py:502
  188.6 21.8 %collective-permute-done.18.refs_0_ = f32[25,2,16,128]{3,2,1,0:T(8,128)S(1)} collective-permute-done((f32[25,2,16,128]{3,2,1,0:T(8,128)S(1)}, f32[25,2,16,128]{3,2,1,0:T(8,128)S(1)}, u32[]{:S(2)}, u32[]{:S(2)}) %collective-permute-start.18) | collective-permute-done | bytes 409632 | tf_op jit(solution)/shard_map/ppermute | solution.py:499
  210.4 3.4 %collective-permute-start.22 = (f32[25,2,16,128]{3,2,1,0:T(8,128)S(1)}, f32[25,2,16,128]{3,2,1,0:T(8,128)S(1)}, u32[]{:S(2)}, u32[]{:S(2)}) collective-permute-start(f32[25,2,16,128]{3,2,1,0:T(8,128)S(1)} %collective-permute-done.18.refs_0_), channel_id=1, source_target_pairs={{0,256},{1,769},{2,258},{3,771},{4,260},{5,773},{6,262},{7,775},{8... | collective-permute-start | bytes 1228808 | tf_op jit(solution)/shard_map/ppermute | solution.py:500
  213.9 3.6 %collective-permute-start.24 = (f32[25,2,16,128]{3,2,1,0:T(8,128)S(1)}, f32[25,2,16,128]{3,2,1,0:T(8,128)S(1)}, u32[]{:S(2)}, u32[]{:S(2)}) collective-permute-start(f32[25,2,16,128]{3,2,1,0:T(8,128)S(1)} %collective-permute-done.18.refs_0_), channel_id=1, source_target_pairs={{0,768},{1,257},{2,770},{3,259},{4,772},{5,261},{6,774},{7,263},{8... | collective-permute-start | bytes 1228808 | tf_op jit(solution)/shard_map/ppermute | solution.py:501
  217.5 4.0 %collective-permute-done.22.refs_1_ = f32[25,2,16,128]{3,2,1,0:T(8,128)S(1)} collective-permute-done((f32[25,2,16,128]{3,2,1,0:T(8,128)S(1)}, f32[25,2,16,128]{3,2,1,0:T(8,128)S(1)}, u32[]{:S(2)}, u32[]{:S(2)}) %collective-permute-start.22) | collective-permute-done | bytes 409632 | tf_op jit(solution)/shard_map/ppermute | solution.py:500
  228.3 4.2 %collective-permute-done.23.refs_2_ = f32[25,2,16,128]{3,2,1,0:T(8,128)S(1)} collective-permute-done((f32[25,2,16,128]{3,2,1,0:T(8,128)S(1)}, f32[25,2,16,128]{3,2,1,0:T(8,128)S(1)}, u32[]{:S(2)}, u32[]{:S(2)}) %collective-permute-start.23) | collective-permute-done | bytes 409632 | tf_op jit(solution)/shard_map/ppermute | solution.py:502
  (43 shorter events, 35.2 us)
Async XLA Ops:
  0.6 61.1 %collective-permute-start = (f32[25,2,16,128]{3,2,1,0:T(8,128)}, f32[25,2,16,128]{3,2,1,0:T(8,128)S(1)}, u32[]{:S(2)}, u32[]{:S(2)}) collective-permute-start(f32[25,2,16,128]{3,2,1,0:T(8,128)} %section.3), channel_id=1, source_target_pairs={{0,1},{1,2},{2,3},{3,4},{4,5},{5,6},{6,7},{7,8},{8,9},{9,10},{10,1... | collective-permute-start | bytes 1228808 | tf_op jit(solution)/shard_map/ppermute | solution.py:518
  2.6 59.1 %collective-permute-start.1 = (f32[25,2,16,128]{3,2,1,0:T(8,128)}, f32[25,2,16,128]{3,2,1,0:T(8,128)S(1)}, u32[]{:S(2)}, u32[]{:S(2)}) collective-permute-start(f32[25,2,16,128]{3,2,1,0:T(8,128)} %section.3), channel_id=1, source_target_pairs={{0,63},{1,0},{2,1},{3,2},{4,3},{5,4},{6,5},{7,6},{8,7},{9,8},{10,9... | collective-permute-start | bytes 1228808 | tf_op jit(solution)/shard_map/ppermute | solution.py:518
  7.5 36.3 %collective-permute-start.4 = (f32[100,128]{1,0:T(8,128)S(1)}, f32[100,128]{1,0:T(8,128)S(1)}, u32[]{:S(2)}, u32[]{:S(2)}) collective-permute-start(f32[100,128]{1,0:T(8,128)S(1)} %get-tuple-element.26), channel_id=1, source_target_pairs={{0,64},{64,128},{128,192},{192,0},{1,65},{65,129},{129,193},{193,1... | collective-permute-start | bytes 153608 | tf_op jit(solution)/shard_map/ppermute | solution.py:518
  23.2 20.6 %collective-permute-start.5 = (f32[100,128]{1,0:T(8,128)S(1)}, f32[100,128]{1,0:T(8,128)S(1)}, u32[]{:S(2)}, u32[]{:S(2)}) collective-permute-start(f32[100,128]{1,0:T(8,128)S(1)} %get-tuple-element.27), channel_id=1, source_target_pairs={{0,192},{64,0},{128,64},{192,128},{1,193},{65,1},{129,65},{193,129... | collective-permute-start | bytes 153608 | tf_op jit(solution)/shard_map/ppermute | solution.py:518
  31.5 6.8 %collective-permute-start.2 = (f32[16,128]{1,0:T(8,128)S(1)}, f32[16,128]{1,0:T(8,128)S(1)}, u32[]{:S(2)}, u32[]{:S(2)}) collective-permute-start(f32[16,128]{1,0:T(8,128)S(1)} %get-tuple-element.24), channel_id=1, source_target_pairs={{0,256},{256,512},{512,768},{768,0},{1,257},{257,513},{513,769},{7... | collective-permute-start | bytes 24584 | tf_op jit(solution)/shard_map/ppermute | solution.py:518
  38.3 5.5 %collective-permute-start.3 = (f32[16,128]{1,0:T(8,128)S(1)}, f32[16,128]{1,0:T(8,128)S(1)}, u32[]{:S(2)}, u32[]{:S(2)}) collective-permute-start(f32[16,128]{1,0:T(8,128)S(1)} %get-tuple-element.25), channel_id=1, source_target_pairs={{0,768},{256,0},{512,256},{768,512},{1,769},{257,1},{513,257},{769... | collective-permute-start | bytes 24584 | tf_op jit(solution)/shard_map/ppermute | solution.py:518
  43.9 17.7 %collective-permute-start.6 = (f32[72,128]{1,0:T(8,128)S(1)}, f32[72,128]{1,0:T(8,128)S(1)}, u32[]{:S(2)}, u32[]{:S(2)}) collective-permute-start(f32[72,128]{1,0:T(8,128)S(1)} %get-tuple-element.28), channel_id=1, source_target_pairs={{0,1},{1,2},{2,3},{3,4},{4,5},{5,6},{6,7},{7,8},{8,9},{9,10},{10,1... | collective-permute-start | bytes 110600 | tf_op jit(solution)/shard_map/ppermute | solution.py:518
  45.9 15.8 %collective-permute-start.7 = (f32[72,128]{1,0:T(8,128)S(1)}, f32[72,128]{1,0:T(8,128)S(1)}, u32[]{:S(2)}, u32[]{:S(2)}) collective-permute-start(f32[72,128]{1,0:T(8,128)S(1)} %get-tuple-element.28), channel_id=1, source_target_pairs={{0,63},{1,0},{2,1},{3,2},{4,3},{5,4},{6,5},{7,6},{8,7},{9,8},{10,9... | collective-permute-start | bytes 110600 | tf_op jit(solution)/shard_map/ppermute | solution.py:518
  49.5 6.7 %collective-permute-start.8 = (f32[4,128]{1,0:T(4,128)S(1)}, f32[4,128]{1,0:T(4,128)S(1)}, u32[]{:S(2)}, u32[]{:S(2)}) collective-permute-start(f32[4,128]{1,0:T(4,128)S(1)} %get-tuple-element.29), channel_id=1, source_target_pairs={{0,256},{256,512},{512,768},{768,0},{1,257},{257,513},{513,769},{7... | collective-permute-start | bytes 6152 | tf_op jit(solution)/shard_map/ppermute | solution.py:518
  72.9 21.1 %collective-permute-start.11 = (f32[25,2,16,128]{3,2,1,0:T(8,128)}, f32[25,2,16,128]{3,2,1,0:T(8,128)S(1)}, u32[]{:S(2)}, u32[]{:S(2)}) collective-permute-start(f32[25,2,16,128]{3,2,1,0:T(8,128)} %get-tuple-element.21.refs_0_), channel_id=1, source_target_pairs={{0,256},{1,769},{2,258},{3,771},{4,260},{5,773},{6,262},{7,775},{8... | collective-permute-start | bytes 1228808 | tf_op jit(solution)/shard_map/ppermute | solution.py:500
  74.8 48.6 %collective-permute-start.10 = (f32[25,2,16,128]{3,2,1,0:T(8,128)}, f32[25,2,16,128]{3,2,1,0:T(8,128)S(1)}, u32[]{:S(2)}, u32[]{:S(2)}) collective-permute-start(f32[25,2,16,128]{3,2,1,0:T(8,128)} %get-tuple-element.21.refs_0_), channel_id=1, source_target_pairs={{0,64},{1,193},{2,66},{3,195},{4,68},{5,197},{6,70},{7,199},{8,72}... | collective-permute-start | bytes 1228808 | tf_op jit(solution)/shard_map/ppermute | solution.py:499
  89.2 34.2 %collective-permute-start.13 = (f32[25,2,16,128]{3,2,1,0:T(8,128)}, f32[25,2,16,128]{3,2,1,0:T(8,128)S(1)}, u32[]{:S(2)}, u32[]{:S(2)}) collective-permute-start(f32[25,2,16,128]{3,2,1,0:T(8,128)} %get-tuple-element.21.refs_0_), channel_id=1, source_target_pairs={{0,768},{1,257},{2,770},{3,259},{4,772},{5,261},{6,774},{7,263},{8... | collective-permute-start | bytes 1228808 | tf_op jit(solution)/shard_map/ppermute | solution.py:501
  94.0 29.4 %collective-permute-start.12 = (f32[25,2,16,128]{3,2,1,0:T(8,128)S(1)}, f32[25,2,16,128]{3,2,1,0:T(8,128)S(1)}, u32[]{:S(2)}, u32[]{:S(2)}) collective-permute-start(f32[25,2,16,128]{3,2,1,0:T(8,128)S(1)} %collective-permute-done.11.refs_1_), channel_id=1, source_target_pairs={{0,256},{1,769},{2,258},{3,771},{4,260},{5,773},{6,262},{7,775},{8... | collective-permute-start | bytes 1228808 | tf_op jit(solution)/shard_map/ppermute | solution.py:502
  123.4 20.9 %collective-permute-start.15 = (f32[25,2,16,128]{3,2,1,0:T(8,128)S(1)}, f32[25,2,16,128]{3,2,1,0:T(8,128)S(1)}, u32[]{:S(2)}, u32[]{:S(2)}) collective-permute-start(f32[25,2,16,128]{3,2,1,0:T(8,128)S(1)} %collective-permute-done.10.refs_0_), channel_id=1, source_target_pairs={{0,256},{1,769},{2,258},{3,771},{4,260},{5,773},{6,262},{7,775},{8... | collective-permute-start | bytes 1228808 | tf_op jit(solution)/shard_map/ppermute | solution.py:500
  126.4 42.9 %collective-permute-start.14 = (f32[25,2,16,128]{3,2,1,0:T(8,128)S(1)}, f32[25,2,16,128]{3,2,1,0:T(8,128)S(1)}, u32[]{:S(2)}, u32[]{:S(2)}) collective-permute-start(f32[25,2,16,128]{3,2,1,0:T(8,128)S(1)} %collective-permute-done.10.refs_0_), channel_id=1, source_target_pairs={{0,64},{1,193},{2,66},{3,195},{4,68},{5,197},{6,70},{7,199},{8,72}... | collective-permute-start | bytes 1228808 | tf_op jit(solution)/shard_map/ppermute | solution.py:499
  139.4 29.9 %collective-permute-start.17 = (f32[25,2,16,128]{3,2,1,0:T(8,128)S(1)}, f32[25,2,16,128]{3,2,1,0:T(8,128)S(1)}, u32[]{:S(2)}, u32[]{:S(2)}) collective-permute-start(f32[25,2,16,128]{3,2,1,0:T(8,128)S(1)} %collective-permute-done.10.refs_0_), channel_id=1, source_target_pairs={{0,768},{1,257},{2,770},{3,259},{4,772},{5,261},{6,774},{7,263},{8... | collective-permute-start | bytes 1228808 | tf_op jit(solution)/shard_map/ppermute | solution.py:501
  144.3 25.0 %collective-permute-start.16 = (f32[25,2,16,128]{3,2,1,0:T(8,128)S(1)}, f32[25,2,16,128]{3,2,1,0:T(8,128)S(1)}, u32[]{:S(2)}, u32[]{:S(2)}) collective-permute-start(f32[25,2,16,128]{3,2,1,0:T(8,128)S(1)} %collective-permute-done.15.refs_1_), channel_id=1, source_target_pairs={{0,256},{1,769},{2,258},{3,771},{4,260},{5,773},{6,262},{7,775},{8... | collective-permute-start | bytes 1228808 | tf_op jit(solution)/shard_map/ppermute | solution.py:502
  169.3 15.1 %collective-permute-start.19 = (f32[25,2,16,128]{3,2,1,0:T(8,128)S(1)}, f32[25,2,16,128]{3,2,1,0:T(8,128)S(1)}, u32[]{:S(2)}, u32[]{:S(2)}) collective-permute-start(f32[25,2,16,128]{3,2,1,0:T(8,128)S(1)} %collective-permute-done.14.refs_0_), channel_id=1, source_target_pairs={{0,256},{1,769},{2,258},{3,771},{4,260},{5,773},{6,262},{7,775},{8... | collective-permute-start | bytes 1228808 | tf_op jit(solution)/shard_map/ppermute | solution.py:500
  172.4 38.0 %collective-permute-start.18 = (f32[25,2,16,128]{3,2,1,0:T(8,128)S(1)}, f32[25,2,16,128]{3,2,1,0:T(8,128)S(1)}, u32[]{:S(2)}, u32[]{:S(2)}) collective-permute-start(f32[25,2,16,128]{3,2,1,0:T(8,128)S(1)} %collective-permute-done.14.refs_0_), channel_id=1, source_target_pairs={{0,64},{1,193},{2,66},{3,195},{4,68},{5,197},{6,70},{7,199},{8,72}... | collective-permute-start | bytes 1228808 | tf_op jit(solution)/shard_map/ppermute | solution.py:499
  179.9 30.5 %collective-permute-start.21 = (f32[25,2,16,128]{3,2,1,0:T(8,128)S(1)}, f32[25,2,16,128]{3,2,1,0:T(8,128)S(1)}, u32[]{:S(2)}, u32[]{:S(2)}) collective-permute-start(f32[25,2,16,128]{3,2,1,0:T(8,128)S(1)} %collective-permute-done.14.refs_0_), channel_id=1, source_target_pairs={{0,768},{1,257},{2,770},{3,259},{4,772},{5,261},{6,774},{7,263},{8... | collective-permute-start | bytes 1228808 | tf_op jit(solution)/shard_map/ppermute | solution.py:501
  184.4 26.1 %collective-permute-start.20 = (f32[25,2,16,128]{3,2,1,0:T(8,128)S(1)}, f32[25,2,16,128]{3,2,1,0:T(8,128)S(1)}, u32[]{:S(2)}, u32[]{:S(2)}) collective-permute-start(f32[25,2,16,128]{3,2,1,0:T(8,128)S(1)} %collective-permute-done.19.refs_1_), channel_id=1, source_target_pairs={{0,256},{1,769},{2,258},{3,771},{4,260},{5,773},{6,262},{7,775},{8... | collective-permute-start | bytes 1228808 | tf_op jit(solution)/shard_map/ppermute | solution.py:502
  210.4 11.0 %collective-permute-start.22 = (f32[25,2,16,128]{3,2,1,0:T(8,128)S(1)}, f32[25,2,16,128]{3,2,1,0:T(8,128)S(1)}, u32[]{:S(2)}, u32[]{:S(2)}) collective-permute-start(f32[25,2,16,128]{3,2,1,0:T(8,128)S(1)} %collective-permute-done.18.refs_0_), channel_id=1, source_target_pairs={{0,256},{1,769},{2,258},{3,771},{4,260},{5,773},{6,262},{7,775},{8... | collective-permute-start | bytes 1228808 | tf_op jit(solution)/shard_map/ppermute | solution.py:500
  213.9 14.5 %collective-permute-start.24 = (f32[25,2,16,128]{3,2,1,0:T(8,128)S(1)}, f32[25,2,16,128]{3,2,1,0:T(8,128)S(1)}, u32[]{:S(2)}, u32[]{:S(2)}) collective-permute-start(f32[25,2,16,128]{3,2,1,0:T(8,128)S(1)} %collective-permute-done.18.refs_0_), channel_id=1, source_target_pairs={{0,768},{1,257},{2,770},{3,259},{4,772},{5,261},{6,774},{7,263},{8... | collective-permute-start | bytes 1228808 | tf_op jit(solution)/shard_map/ppermute | solution.py:501
  221.5 11.0 %collective-permute-start.23 = (f32[25,2,16,128]{3,2,1,0:T(8,128)S(1)}, f32[25,2,16,128]{3,2,1,0:T(8,128)S(1)}, u32[]{:S(2)}, u32[]{:S(2)}) collective-permute-start(f32[25,2,16,128]{3,2,1,0:T(8,128)S(1)} %collective-permute-done.22.refs_1_), channel_id=1, source_target_pairs={{0,256},{1,769},{2,258},{3,771},{4,260},{5,773},{6,262},{7,775},{8... | collective-permute-start | bytes 1228808 | tf_op jit(solution)/shard_map/ppermute | solution.py:502
  (6 other events, 10.5 us)

commit v3 on v2

--- a/solution.py
+++ b/solution.py
@@ -27,7 +27,7 @@
     return lax.broadcasted_iota(jnp.int32, tile.shape, 1)
 
 
-def pack_kernel(section, left, right, top, bottom):
+def pack_kernel(section, held, left, right, top, bottom):
     fields_count, planes, rows, cols = section.shape
     low = jnp.zeros((rows, cols), jnp.float32)
     high = jnp.zeros((rows, cols), jnp.float32)
@@ -36,6 +36,7 @@
         for plane in range(planes):
             number = field * planes + plane
             tile = section[field, plane]
+            held[field, plane] = tile
             low = jnp.where(lane_pair == number, rolled(tile, 2 * number), low)
             high = jnp.where(lane_pair == number, rolled(tile, 2 * number + 2), high)
             top[2 * number : 2 * number + 2, :] = section[field, plane, 0:2, :]
@@ -86,6 +87,9 @@
     return (8.0 / 12.0) * (ahead1 - back1) - (1.0 / 12.0) * (ahead2 - back2)
 
 
+TILE = 8
+
+
 def rate_kernel(
     section,
     below,
@@ -103,101 +107,90 @@
     next_section,
     next_accum,
     ext,
+    side,
     cross_x,
     cross_y,
 ):
     fields_count, planes, rows, _ = section.shape
     last = PAD + rows
+
+    def fill(field, carry):
+        for plane in range(planes):
+            ext[field, plane, PAD:last, :] = below[field, plane]
+            ext[field, planes + plane, PAD:last, :] = section[field, plane]
+            ext[field, 2 * planes + plane, PAD:last, :] = above[field, plane]
+        return carry
+
+    lax.fori_loop(0, fields_count, fill, 0)
     for field in range(fields_count):
         for plane in range(planes):
-            number = 2 * (field * planes + plane)
-            ext[field, plane, PAD:last, :] = section[field, plane]
-            ext[field, plane, PAD - 2 : PAD, :] = from_low[number : number + 2, :]
-            ext[field, plane, last : last + 2, :] = from_high[number : number + 2, :]
-
-    def layer(field, plane):
-        if plane < 0:
-            return below[field, plane + 2]
-        if plane > 1:
-            return above[field, plane - 2]
-        return section[field, plane]
-
+            number = field * planes + plane
+            side[field, plane] = border(from_left[...], from_right[...], number)
+            place = 2 * number
+            ext[field, plane + 2, PAD - 2 : PAD, :] = from_low[place : place + 2, :]
+            ext[field, plane + 2, last : last + 2, :] = from_high[place : place + 2, :]
     for slot, field in enumerate(EDGED):
-        for plane in range(-2, 4):
-            tile = layer(field, plane)
-            if plane in (0, 1):
-                edge = border(from_left[...], from_right[...], 2 * field + plane)
-                cross_x[slot, plane + 2, PAD:last, :] = slope(along_lanes(tile, edge))
-                for side, place in enumerate((PAD - 2, last)):
-                    strip = ext[field, plane, place : place + 2, :]
-                    edge = border(
-                        corner_left[2 * side : 2 * side + 2, :],
-                        corner_right[2 * side : 2 * side + 2, :],
-                        2 * slot + plane,
+        for layer in range(6):
+            if layer in (2, 3):
+                edge = side[field, layer - 2]
+                for number, place in enumerate((PAD - 2, last)):
+                    strip = border(
+                        corner_left[2 * number : 2 * number + 2, :],
+                        corner_right[2 * number : 2 * number + 2, :],
+                        2 * slot + layer - 2,
                     )
-                    cross_x[slot, plane + 2, place : place + 2, :] = slope(
-                        along_lanes(strip, edge)
+                    cross_x[slot, layer, place : place + 2, :] = slope(
+                        along_lanes(ext[field, layer, place : place + 2, :], strip)
                     )
-                column = ext.at[field, plane]
             else:
-                source, local = (edges_below, plane + 2) if plane < 0 else (edges_above, plane - 2)
+                source, local = (edges_below, layer) if layer < 2 else (edges_above, layer - 4)
                 edge = border(source[0:16, :], source[16:32, :], 2 * field + local)
-                cross_x[slot, plane + 2, PAD:last, :] = slope(along_lanes(tile, edge))
                 place = 4 * slot + 2 * local
-                depth = fields_count + (plane + 2 if plane < 0 else plane)
-                column = ext.at[depth, slot % 2]
-                column[PAD:last, :] = tile
-                column[PAD - 2 : PAD, :] = source[32 + place : 34 + place, :]
-                column[last : last + 2, :] = source[52 + place : 54 + place, :]
-            cross_y[slot, plane + 2] = slope(
-                tuple(column[PAD + off : last + off, :] for off in (-2, -1, 1, 2))
-            )
-
-    for plane in range(planes):
+                ext[field, layer, PAD - 2 : PAD, :] = source[32 + place : 34 + place, :]
+                ext[field, layer, last : last + 2, :] = source[52 + place : 54 + place, :]
+            cross_x[slot, layer, PAD:last, :] = slope(
+                along_lanes(ext[field, layer, PAD:last, :], edge)
+            )
+
+    def tilt(number, carry):
+        slot = number // 6
+        layer = number % 6
+        field = jnp.where(slot == 0, 0, slot + 16)
+        cross_y[slot, layer] = slope(
+            tuple(ext[field, layer, PAD + off : last + off, :] for off in (-2, -1, 1, 2))
+        )
+        return carry
+
+    lax.fori_loop(0, 30, tilt, 0)
+
+    def tile_rates(number, carry):
         write_rates(
-            plane,
-            section,
-            layer,
-            from_left,
-            from_right,
-            base,
-            accum,
-            next_section,
-            next_accum,
-            ext,
-            cross_x,
-            cross_y,
-        )
-
-
-def write_rates(
-    plane,
-    section,
-    layer,
-    from_left,
-    from_right,
-    base,
-    accum,
-    next_section,
-    next_accum,
-    ext,
-    cross_x,
-    cross_y,
-):
-    rows = section.shape[2]
-    last = PAD + rows
-    centre = [section[field, plane] for field in range(25)]
+            number, side, base, accum, next_section, next_accum, ext, cross_x, cross_y
+        )
+        return carry
+
+    lax.fori_loop(0, planes * rows // TILE, tile_rates, 0)
+
+
+def write_rates(number, side, base, accum, next_section, next_accum, ext, cross_x, cross_y):
+    parts = 16 // TILE
+    plane = number // parts
+    start = 0 if parts == 1 else pl.multiple_of((number % parts) * TILE, TILE)
+
+    def span(begin):
+        if parts == 1:
+            return slice(begin, begin + TILE)
+        return pl.ds(start + begin, TILE)
+
+    centre = [ext[field, plane + 2, span(PAD), :] for field in range(25)]
     gradients = [[None] * 25 for _ in range(3)]
     curves = [[None] * 25 for _ in range(3)]
     smoothing = [None] * 25
     for field in range(25):
         tile = centre[field]
-        edge = border(from_left[...], from_right[...], 2 * field + plane)
-        around_x = along_lanes(tile, edge)
-        around_y = tuple(
-            ext[field, plane, PAD + off : last + off, :] for off in (-2, -1, 1, 2)
-        )
-        around_z = tuple(layer(field, plane + off) for off in (-2, -1, 1, 2))
+        around_x = along_lanes(tile, side[field, plane, span(0), :])
+        around_y = tuple(ext[field, plane + 2, span(PAD + off), :] for off in (-2, -1, 1, 2))
+        around_z = tuple(ext[field, plane + 2 + off, span(PAD), :] for off in (-2, -1, 1, 2))
         total_near, total_far = None, None
         for direction, around in enumerate((around_x, around_y, around_z)):
             back2, back1, ahead1, ahead2 = around
@@ -211,30 +204,26 @@
             total_far = far if total_far is None else total_far + far
         smoothing[field] = total_far - 4.0 * total_near + 18.0 * tile
     mixed_terms = {(0, 1): [], (0, 2): [], (1, 2): []}
+    offsets = (-2, -1, 1, 2)
     for slot in range(5):
         mixed_terms[0, 1].append(
-            slope(
-                tuple(
-                    cross_x[slot, plane + 2, PAD + off : last + off, :]
-                    for off in (-2, -1, 1, 2)
-                )
-            )
+            slope(tuple(cross_x[slot, plane + 2, span(PAD + off), :] for off in offsets))
         )
         mixed_terms[0, 2].append(
-            slope(
-                tuple(
-                    cross_x[slot, plane + 2 + off, PAD:last, :] for off in (-2, -1, 1, 2)
-                )
-            )
+            slope(tuple(cross_x[slot, plane + 2 + off, span(PAD), :] for off in offsets))
         )
         mixed_terms[1, 2].append(
-            slope(tuple(cross_y[slot, plane + 2 + off] for off in (-2, -1, 1, 2)))
+            slope(tuple(cross_y[slot, plane + 2 + off, span(0), :] for off in offsets))
         )
     rates = evolve_rate(centre, gradients, curves, mixed_terms)
     for field in range(25):
         rate = rates[field] + (-DISSIPATE / 16.0) * smoothing[field]
-        next_section[field, plane] = base[field, plane] + (0.5 * STEP_DT) * rate
-        next_accum[field, plane] = accum[field, plane] + (STEP_DT / 3.0) * rate
+        next_section[field, plane, span(0), :] = (
+            base[field, plane, span(0), :] + (0.5 * STEP_DT) * rate
+        )
+        next_accum[field, plane, span(0), :] = (
+            accum[field, plane, span(0), :] + (STEP_DT / 3.0) * rate
+        )
 
 
 def evolve_rate(centre, gradients, curves, mixed_terms):
@@ -529,11 +518,11 @@
     block = jax.ShapeDtypeStruct(section.shape, jnp.float32)
     below = sent(section, "gz", 1)
     above = sent(section, "gz", -1)
-    left, right, top, bottom = pl.pallas_call(
+    held, left, right, top, bottom = pl.pallas_call(
         pack_kernel,
-        out_shape=(flat, flat, strip, strip),
+        out_shape=(block, flat, flat, strip, strip),
         in_specs=vmem(1),
-        out_specs=tuple(vmem(4)),
+        out_specs=tuple(vmem(5)),
         compiler_params=pltpu.CompilerParams(vmem_limit_bytes=4 * 1024 * 1024),
         cost_estimate=pl.CostEstimate(flops=2000000, bytes_accessed=600000, transcendentals=0),
         name="pack",
@@ -561,7 +550,8 @@
         in_specs=vmem(13),
         out_specs=tuple(vmem(2)),
         scratch_shapes=[
-            pltpu.VMEM((29, 2, 32, 128), jnp.float32),
+            pltpu.VMEM((25, 6, 32, 128), jnp.float32),
+            pltpu.VMEM((25, 2, 16, 128), jnp.float32),
             pltpu.VMEM((5, 6, 32, 128), jnp.float32),
             pltpu.VMEM((5, 6, 16, 128), jnp.float32),
         ],
@@ -569,7 +559,7 @@
         cost_estimate=pl.CostEstimate(flops=30000000, bytes_accessed=3000000, transcendentals=0),
         name="rate",
     )(
-        section,
+        held,
         below,
         above,
         from_left,

time: 235 us -> 232 us (0.987)
    unnamed x10 -> x8, local copies, waits for them, and re-layouts: 5 us -> 4 us
where the time goes in v3:
time: 232 us; the launch traced here: 231 us
  starting transfers between devices  124 us (53%)
  waiting for transfers between devices  90.5 us (39%)
  Pallas kernels  11.2 us (5%)
  local copies, waits for them, and re-layouts  4 us (2%)
    ppermute x3, waiting for transfers between devices, slab_of(): following = lax.ppermute(current, AXES, along_y)  71.1 us
    ppermute x10, starting transfers between devices, sent(): return lax.ppermute(array, axis, ring(axis, step))  48.3 us
    ppermute x3, starting transfers between devices, slab_of(): following = lax.ppermute(current, AXES, along_y)  35 us
    ppermute x4, starting transfers between devices, slab_of(): back = lax.ppermute(current, AXES, against_x)  17.7 us
    ppermute x4, starting transfers between devices, slab_of(): second = lax.ppermute(first, AXES, along_x)  11.5 us
    ppermute x4, starting transfers between devices, slab_of(): first = lax.ppermute(current, AXES, along_x)  11.4 us
    ppermute x10, waiting for transfers between devices, sent(): return lax.ppermute(array, axis, ring(axis, step))  11.3 us
    pallas_call x1, Pallas kernels, shards(): pl.pallas_call(rate_kernel, out_shape=(block, block), in_specs=vmem(13),...  6.02 us
  transfers between devices with their start and end apart: 25, of which 9 were waited for; matrix products, arithmetic and copies ran while one was open for 0% of the time, Pallas kernels for 2%

profile of v3, /device:TPU:38, one launch (start us, length us, event | category | flops | bytes accessed | tf_op | source)
XLA Modules:
  0.0 230.6 jit_solution(17839708445933661746)
XLA Ops:
  2.6 3.6 %collective-permute-start.1 = (f32[25,2,16,128]{3,2,1,0:T(8,128)}, f32[25,2,16,128]{3,2,1,0:T(8,128)S(1)}, u32[]{:S(2)}, u32[]{:S(2)}) collective-permute-start(f32[25,2,16,128]{3,2,1,0:T(8,128)} %section.1), channel_id=1, source_target_pairs={{0,63},{1,0},{2,1},{3,2},{4,3},{5,4},{6,5},{7,6},{8,7},{9,8},{10,9... | collective-permute-start | bytes 1228808 | tf_op jit(solution)/shard_map/ppermute | solution.py:507
  7.5 15.7 %collective-permute-start.4 = (f32[100,128]{1,0:T(8,128)S(1)}, f32[100,128]{1,0:T(8,128)S(1)}, u32[]{:S(2)}, u32[]{:S(2)}) collective-permute-start(f32[100,128]{1,0:T(8,128)S(1)} %get-tuple-element.28), channel_id=1, source_target_pairs={{0,64},{64,128},{128,192},{192,0},{1,65},{65,129},{129,193},{193,1... | collective-permute-start | bytes 153608 | tf_op jit(solution)/shard_map/ppermute | solution.py:507
  23.2 8.3 %collective-permute-start.5 = (f32[100,128]{1,0:T(8,128)S(1)}, f32[100,128]{1,0:T(8,128)S(1)}, u32[]{:S(2)}, u32[]{:S(2)}) collective-permute-start(f32[100,128]{1,0:T(8,128)S(1)} %get-tuple-element.29), channel_id=1, source_target_pairs={{0,192},{64,0},{128,64},{192,128},{1,193},{65,1},{129,65},{193,129... | collective-permute-start | bytes 153608 | tf_op jit(solution)/shard_map/ppermute | solution.py:507
  31.5 3.5 %collective-permute-start.2 = (f32[16,128]{1,0:T(8,128)S(1)}, f32[16,128]{1,0:T(8,128)S(1)}, u32[]{:S(2)}, u32[]{:S(2)}) collective-permute-start(f32[16,128]{1,0:T(8,128)S(1)} %get-tuple-element.26), channel_id=1, source_target_pairs={{0,256},{256,512},{512,768},{768,0},{1,257},{257,513},{513,769},{7... | collective-permute-start | bytes 24584 | tf_op jit(solution)/shard_map/ppermute | solution.py:507
  35.0 3.3 %collective-permute-done.2.from_left = f32[16,128]{1,0:T(8,128)S(1)} collective-permute-done((f32[16,128]{1,0:T(8,128)S(1)}, f32[16,128]{1,0:T(8,128)S(1)}, u32[]{:S(2)}, u32[]{:S(2)}) %collective-permute-start.2) | collective-permute-done | bytes 8224 | tf_op jit(solution)/shard_map/ppermute | solution.py:507
  38.3 3.7 %collective-permute-start.3 = (f32[16,128]{1,0:T(8,128)S(1)}, f32[16,128]{1,0:T(8,128)S(1)}, u32[]{:S(2)}, u32[]{:S(2)}) collective-permute-start(f32[16,128]{1,0:T(8,128)S(1)} %get-tuple-element.27), channel_id=1, source_target_pairs={{0,768},{256,0},{512,256},{768,512},{1,769},{257,1},{513,257},{769... | collective-permute-start | bytes 24584 | tf_op jit(solution)/shard_map/ppermute | solution.py:507
  45.9 3.6 %collective-permute-start.7 = (f32[72,128]{1,0:T(8,128)S(1)}, f32[72,128]{1,0:T(8,128)S(1)}, u32[]{:S(2)}, u32[]{:S(2)}) collective-permute-start(f32[72,128]{1,0:T(8,128)S(1)} %get-tuple-element.30), channel_id=1, source_target_pairs={{0,63},{1,0},{2,1},{3,2},{4,3},{5,4},{6,5},{7,6},{8,7},{9,8},{10,9... | collective-permute-start | bytes 110600 | tf_op jit(solution)/shard_map/ppermute | solution.py:507
  51.8 4.4 %collective-permute-done.8.corner_left = f32[4,128]{1,0:T(4,128)S(1)} collective-permute-done((f32[4,128]{1,0:T(4,128)S(1)}, f32[4,128]{1,0:T(4,128)S(1)}, u32[]{:S(2)}, u32[]{:S(2)}) %collective-permute-start.8) | collective-permute-done | bytes 2080 | tf_op jit(solution)/shard_map/ppermute | solution.py:507
  56.2 3.7 %collective-permute-start.9 = (f32[4,128]{1,0:T(4,128)S(1)}, f32[4,128]{1,0:T(4,128)S(1)}, u32[]{:S(2)}, u32[]{:S(2)}) collective-permute-start(f32[4,128]{1,0:T(4,128)S(1)} %get-tuple-element.32), channel_id=1, source_target_pairs={{0,768},{256,0},{512,256},{768,512},{1,769},{257,1},{513,257},{769... | collective-permute-start | bytes 6152 | tf_op jit(solution)/shard_map/ppermute | solution.py:507
  63.7 6.0 %rate.1 = (f32[25,2,16,128]{3,2,1,0:T(8,128)}, f32[25,2,16,128]{3,2,1,0:T(8,128)}) custom-call(f32[25,2,16,128]{3,2,1,0:T(8,128)S(1)} %get-tuple-element.25.section, f32[25,2,16,128]{3,2,1,0:T(8,128)S(1)} %collective-permute-done.below, f32[25,2,16,128]{3,2,1,0:T(8,128)S(1)} %collective-permute-done.1.above, f32[16,128]{1,0:T(8,128)S(1)} %collective-permute-done.2.from_left, ...), custom_call_target="tpu_custom_call" | custom-call | flops 30000000 | bytes 3000000 | tf_op jit(solution)/shard_map/rate/pallas_call | solution.py:547
  71.6 14.4 %collective-permute-start.10 = (f32[25,2,16,128]{3,2,1,0:T(8,128)}, f32[25,2,16,128]{3,2,1,0:T(8,128)S(1)}, u32[]{:S(2)}, u32[]{:S(2)}) collective-permute-start(f32[25,2,16,128]{3,2,1,0:T(8,128)} %get-tuple-element.22.refs_0_), channel_id=1, source_target_pairs={{0,64},{1,193},{2,66},{3,195},{4,68},{5,197},{6,70},{7,199},{8,72}... | collective-permute-start | bytes 1228808 | tf_op jit(solution)/shard_map/ppermute | solution.py:488
  86.1 4.8 %collective-permute-start.13 = (f32[25,2,16,128]{3,2,1,0:T(8,128)}, f32[25,2,16,128]{3,2,1,0:T(8,128)S(1)}, u32[]{:S(2)}, u32[]{:S(2)}) collective-permute-start(f32[25,2,16,128]{3,2,1,0:T(8,128)} %get-tuple-element.22.refs_0_), channel_id=1, source_target_pairs={{0,768},{1,257},{2,770},{3,259},{4,772},{5,261},{6,774},{7,263},{8... | collective-permute-start | bytes 1228808 | tf_op jit(solution)/shard_map/ppermute | solution.py:490
  92.8 27.4 %collective-permute-done.10.refs_0_ = f32[25,2,16,128]{3,2,1,0:T(8,128)S(1)} collective-permute-done((f32[25,2,16,128]{3,2,1,0:T(8,128)}, f32[25,2,16,128]{3,2,1,0:T(8,128)S(1)}, u32[]{:S(2)}, u32[]{:S(2)}) %collective-permute-start.10) | collective-permute-done | bytes 409632 | tf_op jit(solution)/shard_map/ppermute | solution.py:488
  123.2 13.1 %collective-permute-start.14 = (f32[25,2,16,128]{3,2,1,0:T(8,128)S(1)}, f32[25,2,16,128]{3,2,1,0:T(8,128)S(1)}, u32[]{:S(2)}, u32[]{:S(2)}) collective-permute-start(f32[25,2,16,128]{3,2,1,0:T(8,128)S(1)} %collective-permute-done.10.refs_0_), channel_id=1, source_target_pairs={{0,64},{1,193},{2,66},{3,195},{4,68},{5,197},{6,70},{7,199},{8,72}... | collective-permute-start | bytes 1228808 | tf_op jit(solution)/shard_map/ppermute | solution.py:488
  136.3 4.8 %collective-permute-start.17 = (f32[25,2,16,128]{3,2,1,0:T(8,128)S(1)}, f32[25,2,16,128]{3,2,1,0:T(8,128)S(1)}, u32[]{:S(2)}, u32[]{:S(2)}) collective-permute-start(f32[25,2,16,128]{3,2,1,0:T(8,128)S(1)} %collective-permute-done.10.refs_0_), channel_id=1, source_target_pairs={{0,768},{1,257},{2,770},{3,259},{4,772},{5,261},{6,774},{7,263},{8... | collective-permute-start | bytes 1228808 | tf_op jit(solution)/shard_map/ppermute | solution.py:490
  144.3 21.8 %collective-permute-done.14.refs_0_ = f32[25,2,16,128]{3,2,1,0:T(8,128)S(1)} collective-permute-done((f32[25,2,16,128]{3,2,1,0:T(8,128)S(1)}, f32[25,2,16,128]{3,2,1,0:T(8,128)S(1)}, u32[]{:S(2)}, u32[]{:S(2)}) %collective-permute-start.14) | collective-permute-done | bytes 409632 | tf_op jit(solution)/shard_map/ppermute | solution.py:488
  169.2 7.5 %collective-permute-start.18 = (f32[25,2,16,128]{3,2,1,0:T(8,128)S(1)}, f32[25,2,16,128]{3,2,1,0:T(8,128)S(1)}, u32[]{:S(2)}, u32[]{:S(2)}) collective-permute-start(f32[25,2,16,128]{3,2,1,0:T(8,128)S(1)} %collective-permute-done.14.refs_0_), channel_id=1, source_target_pairs={{0,64},{1,193},{2,66},{3,195},{4,68},{5,197},{6,70},{7,199},{8,72}... | collective-permute-start | bytes 1228808 | tf_op jit(solution)/shard_map/ppermute | solution.py:488
  176.8 4.4 %collective-permute-start.21 = (f32[25,2,16,128]{3,2,1,0:T(8,128)S(1)}, f32[25,2,16,128]{3,2,1,0:T(8,128)S(1)}, u32[]{:S(2)}, u32[]{:S(2)}) collective-permute-start(f32[25,2,16,128]{3,2,1,0:T(8,128)S(1)} %collective-permute-done.14.refs_0_), channel_id=1, source_target_pairs={{0,768},{1,257},{2,770},{3,259},{4,772},{5,261},{6,774},{7,263},{8... | collective-permute-start | bytes 1228808 | tf_op jit(solution)/shard_map/ppermute | solution.py:490
  181.2 4.2 %collective-permute-start.20 = (f32[25,2,16,128]{3,2,1,0:T(8,128)S(1)}, f32[25,2,16,128]{3,2,1,0:T(8,128)S(1)}, u32[]{:S(2)}, u32[]{:S(2)}) collective-permute-start(f32[25,2,16,128]{3,2,1,0:T(8,128)S(1)} %collective-permute-done.19.refs_1_), channel_id=1, source_target_pairs={{0,256},{1,769},{2,258},{3,771},{4,260},{5,773},{6,262},{7,775},{8... | collective-permute-start | bytes 1228808 | tf_op jit(solution)/shard_map/ppermute | solution.py:491
  185.5 21.8 %collective-permute-done.18.refs_0_ = f32[25,2,16,128]{3,2,1,0:T(8,128)S(1)} collective-permute-done((f32[25,2,16,128]{3,2,1,0:T(8,128)S(1)}, f32[25,2,16,128]{3,2,1,0:T(8,128)S(1)}, u32[]{:S(2)}, u32[]{:S(2)}) %collective-permute-start.18) | collective-permute-done | bytes 409632 | tf_op jit(solution)/shard_map/ppermute | solution.py:488
  207.3 3.4 %collective-permute-start.22 = (f32[25,2,16,128]{3,2,1,0:T(8,128)S(1)}, f32[25,2,16,128]{3,2,1,0:T(8,128)S(1)}, u32[]{:S(2)}, u32[]{:S(2)}) collective-permute-start(f32[25,2,16,128]{3,2,1,0:T(8,128)S(1)} %collective-permute-done.18.refs_0_), channel_id=1, source_target_pairs={{0,256},{1,769},{2,258},{3,771},{4,260},{5,773},{6,262},{7,775},{8... | collective-permute-start | bytes 1228808 | tf_op jit(solution)/shard_map/ppermute | solution.py:489
  210.7 3.6 %collective-permute-start.24 = (f32[25,2,16,128]{3,2,1,0:T(8,128)S(1)}, f32[25,2,16,128]{3,2,1,0:T(8,128)S(1)}, u32[]{:S(2)}, u32[]{:S(2)}) collective-permute-start(f32[25,2,16,128]{3,2,1,0:T(8,128)S(1)} %collective-permute-done.18.refs_0_), channel_id=1, source_target_pairs={{0,768},{1,257},{2,770},{3,259},{4,772},{5,261},{6,774},{7,263},{8... | collective-permute-start | bytes 1228808 | tf_op jit(solution)/shard_map/ppermute | solution.py:490
  214.4 4.0 %collective-permute-done.22.refs_1_ = f32[25,2,16,128]{3,2,1,0:T(8,128)S(1)} collective-permute-done((f32[25,2,16,128]{3,2,1,0:T(8,128)S(1)}, f32[25,2,16,128]{3,2,1,0:T(8,128)S(1)}, u32[]{:S(2)}, u32[]{:S(2)}) %collective-permute-start.22) | collective-permute-done | bytes 409632 | tf_op jit(solution)/shard_map/ppermute | solution.py:489
  225.2 4.2 %collective-permute-done.23.refs_2_ = f32[25,2,16,128]{3,2,1,0:T(8,128)S(1)} collective-permute-done((f32[25,2,16,128]{3,2,1,0:T(8,128)S(1)}, f32[25,2,16,128]{3,2,1,0:T(8,128)S(1)}, u32[]{:S(2)}, u32[]{:S(2)}) %collective-permute-start.23) | collective-permute-done | bytes 409632 | tf_op jit(solution)/shard_map/ppermute | solution.py:491
  (41 shorter events, 34.2 us)
Async XLA Ops:
  0.6 61.1 %collective-permute-start = (f32[25,2,16,128]{3,2,1,0:T(8,128)}, f32[25,2,16,128]{3,2,1,0:T(8,128)S(1)}, u32[]{:S(2)}, u32[]{:S(2)}) collective-permute-start(f32[25,2,16,128]{3,2,1,0:T(8,128)} %section.1), channel_id=1, source_target_pairs={{0,1},{1,2},{2,3},{3,4},{4,5},{5,6},{6,7},{7,8},{8,9},{9,10},{10,1... | collective-permute-start | bytes 1228808 | tf_op jit(solution)/shard_map/ppermute | solution.py:507
  2.6 59.1 %collective-permute-start.1 = (f32[25,2,16,128]{3,2,1,0:T(8,128)}, f32[25,2,16,128]{3,2,1,0:T(8,128)S(1)}, u32[]{:S(2)}, u32[]{:S(2)}) collective-permute-start(f32[25,2,16,128]{3,2,1,0:T(8,128)} %section.1), channel_id=1, source_target_pairs={{0,63},{1,0},{2,1},{3,2},{4,3},{5,4},{6,5},{7,6},{8,7},{9,8},{10,9... | collective-permute-start | bytes 1228808 | tf_op jit(solution)/shard_map/ppermute | solution.py:507
  7.5 36.3 %collective-permute-start.4 = (f32[100,128]{1,0:T(8,128)S(1)}, f32[100,128]{1,0:T(8,128)S(1)}, u32[]{:S(2)}, u32[]{:S(2)}) collective-permute-start(f32[100,128]{1,0:T(8,128)S(1)} %get-tuple-element.28), channel_id=1, source_target_pairs={{0,64},{64,128},{128,192},{192,0},{1,65},{65,129},{129,193},{193,1... | collective-permute-start | bytes 153608 | tf_op jit(solution)/shard_map/ppermute | solution.py:507
  23.2 20.6 %collective-permute-start.5 = (f32[100,128]{1,0:T(8,128)S(1)}, f32[100,128]{1,0:T(8,128)S(1)}, u32[]{:S(2)}, u32[]{:S(2)}) collective-permute-start(f32[100,128]{1,0:T(8,128)S(1)} %get-tuple-element.29), channel_id=1, source_target_pairs={{0,192},{64,0},{128,64},{192,128},{1,193},{65,1},{129,65},{193,129... | collective-permute-start | bytes 153608 | tf_op jit(solution)/shard_map/ppermute | solution.py:507
  31.5 6.8 %collective-permute-start.2 = (f32[16,128]{1,0:T(8,128)S(1)}, f32[16,128]{1,0:T(8,128)S(1)}, u32[]{:S(2)}, u32[]{:S(2)}) collective-permute-start(f32[16,128]{1,0:T(8,128)S(1)} %get-tuple-element.26), channel_id=1, source_target_pairs={{0,256},{256,512},{512,768},{768,0},{1,257},{257,513},{513,769},{7... | collective-permute-start | bytes 24584 | tf_op jit(solution)/shard_map/ppermute | solution.py:507
  38.3 5.5 %collective-permute-start.3 = (f32[16,128]{1,0:T(8,128)S(1)}, f32[16,128]{1,0:T(8,128)S(1)}, u32[]{:S(2)}, u32[]{:S(2)}) collective-permute-start(f32[16,128]{1,0:T(8,128)S(1)} %get-tuple-element.27), channel_id=1, source_target_pairs={{0,768},{256,0},{512,256},{768,512},{1,769},{257,1},{513,257},{769... | collective-permute-start | bytes 24584 | tf_op jit(solution)/shard_map/ppermute | solution.py:507
  43.9 17.7 %collective-permute-start.6 = (f32[72,128]{1,0:T(8,128)S(1)}, f32[72,128]{1,0:T(8,128)S(1)}, u32[]{:S(2)}, u32[]{:S(2)}) collective-permute-start(f32[72,128]{1,0:T(8,128)S(1)} %get-tuple-element.30), channel_id=1, source_target_pairs={{0,1},{1,2},{2,3},{3,4},{4,5},{5,6},{6,7},{7,8},{8,9},{9,10},{10,1... | collective-permute-start | bytes 110600 | tf_op jit(solution)/shard_map/ppermute | solution.py:507
  45.9 15.8 %collective-permute-start.7 = (f32[72,128]{1,0:T(8,128)S(1)}, f32[72,128]{1,0:T(8,128)S(1)}, u32[]{:S(2)}, u32[]{:S(2)}) collective-permute-start(f32[72,128]{1,0:T(8,128)S(1)} %get-tuple-element.30), channel_id=1, source_target_pairs={{0,63},{1,0},{2,1},{3,2},{4,3},{5,4},{6,5},{7,6},{8,7},{9,8},{10,9... | collective-permute-start | bytes 110600 | tf_op jit(solution)/shard_map/ppermute | solution.py:507
  49.5 6.7 %collective-permute-start.8 = (f32[4,128]{1,0:T(4,128)S(1)}, f32[4,128]{1,0:T(4,128)S(1)}, u32[]{:S(2)}, u32[]{:S(2)}) collective-permute-start(f32[4,128]{1,0:T(4,128)S(1)} %get-tuple-element.31), channel_id=1, source_target_pairs={{0,256},{256,512},{512,768},{768,0},{1,257},{257,513},{513,769},{7... | collective-permute-start | bytes 6152 | tf_op jit(solution)/shard_map/ppermute | solution.py:507
  69.7 21.1 %collective-permute-start.11 = (f32[25,2,16,128]{3,2,1,0:T(8,128)}, f32[25,2,16,128]{3,2,1,0:T(8,128)S(1)}, u32[]{:S(2)}, u32[]{:S(2)}) collective-permute-start(f32[25,2,16,128]{3,2,1,0:T(8,128)} %get-tuple-element.22.refs_0_), channel_id=1, source_target_pairs={{0,256},{1,769},{2,258},{3,771},{4,260},{5,773},{6,262},{7,775},{8... | collective-permute-start | bytes 1228808 | tf_op jit(solution)/shard_map/ppermute | solution.py:489
  71.6 48.6 %collective-permute-start.10 = (f32[25,2,16,128]{3,2,1,0:T(8,128)}, f32[25,2,16,128]{3,2,1,0:T(8,128)S(1)}, u32[]{:S(2)}, u32[]{:S(2)}) collective-permute-start(f32[25,2,16,128]{3,2,1,0:T(8,128)} %get-tuple-element.22.refs_0_), channel_id=1, source_target_pairs={{0,64},{1,193},{2,66},{3,195},{4,68},{5,197},{6,70},{7,199},{8,72}... | collective-permute-start | bytes 1228808 | tf_op jit(solution)/shard_map/ppermute | solution.py:488
  86.1 34.2 %collective-permute-start.13 = (f32[25,2,16,128]{3,2,1,0:T(8,128)}, f32[25,2,16,128]{3,2,1,0:T(8,128)S(1)}, u32[]{:S(2)}, u32[]{:S(2)}) collective-permute-start(f32[25,2,16,128]{3,2,1,0:T(8,128)} %get-tuple-element.22.refs_0_), channel_id=1, source_target_pairs={{0,768},{1,257},{2,770},{3,259},{4,772},{5,261},{6,774},{7,263},{8... | collective-permute-start | bytes 1228808 | tf_op jit(solution)/shard_map/ppermute | solution.py:490
  90.9 29.4 %collective-permute-start.12 = (f32[25,2,16,128]{3,2,1,0:T(8,128)S(1)}, f32[25,2,16,128]{3,2,1,0:T(8,128)S(1)}, u32[]{:S(2)}, u32[]{:S(2)}) collective-permute-start(f32[25,2,16,128]{3,2,1,0:T(8,128)S(1)} %collective-permute-done.11.refs_1_), channel_id=1, source_target_pairs={{0,256},{1,769},{2,258},{3,771},{4,260},{5,773},{6,262},{7,775},{8... | collective-permute-start | bytes 1228808 | tf_op jit(solution)/shard_map/ppermute | solution.py:491
  120.2 20.9 %collective-permute-start.15 = (f32[25,2,16,128]{3,2,1,0:T(8,128)S(1)}, f32[25,2,16,128]{3,2,1,0:T(8,128)S(1)}, u32[]{:S(2)}, u32[]{:S(2)}) collective-permute-start(f32[25,2,16,128]{3,2,1,0:T(8,128)S(1)} %collective-permute-done.10.refs_0_), channel_id=1, source_target_pairs={{0,256},{1,769},{2,258},{3,771},{4,260},{5,773},{6,262},{7,775},{8... | collective-permute-start | bytes 1228808 | tf_op jit(solution)/shard_map/ppermute | solution.py:489
  123.2 42.9 %collective-permute-start.14 = (f32[25,2,16,128]{3,2,1,0:T(8,128)S(1)}, f32[25,2,16,128]{3,2,1,0:T(8,128)S(1)}, u32[]{:S(2)}, u32[]{:S(2)}) collective-permute-start(f32[25,2,16,128]{3,2,1,0:T(8,128)S(1)} %collective-permute-done.10.refs_0_), channel_id=1, source_target_pairs={{0,64},{1,193},{2,66},{3,195},{4,68},{5,197},{6,70},{7,199},{8,72}... | collective-permute-start | bytes 1228808 | tf_op jit(solution)/shard_map/ppermute | solution.py:488
  136.3 29.9 %collective-permute-start.17 = (f32[25,2,16,128]{3,2,1,0:T(8,128)S(1)}, f32[25,2,16,128]{3,2,1,0:T(8,128)S(1)}, u32[]{:S(2)}, u32[]{:S(2)}) collective-permute-start(f32[25,2,16,128]{3,2,1,0:T(8,128)S(1)} %collective-permute-done.10.refs_0_), channel_id=1, source_target_pairs={{0,768},{1,257},{2,770},{3,259},{4,772},{5,261},{6,774},{7,263},{8... | collective-permute-start | bytes 1228808 | tf_op jit(solution)/shard_map/ppermute | solution.py:490
  141.2 25.0 %collective-permute-start.16 = (f32[25,2,16,128]{3,2,1,0:T(8,128)S(1)}, f32[25,2,16,128]{3,2,1,0:T(8,128)S(1)}, u32[]{:S(2)}, u32[]{:S(2)}) collective-permute-start(f32[25,2,16,128]{3,2,1,0:T(8,128)S(1)} %collective-permute-done.15.refs_1_), channel_id=1, source_target_pairs={{0,256},{1,769},{2,258},{3,771},{4,260},{5,773},{6,262},{7,775},{8... | collective-permute-start | bytes 1228808 | tf_op jit(solution)/shard_map/ppermute | solution.py:491
  166.2 15.1 %collective-permute-start.19 = (f32[25,2,16,128]{3,2,1,0:T(8,128)S(1)}, f32[25,2,16,128]{3,2,1,0:T(8,128)S(1)}, u32[]{:S(2)}, u32[]{:S(2)}) collective-permute-start(f32[25,2,16,128]{3,2,1,0:T(8,128)S(1)} %collective-permute-done.14.refs_0_), channel_id=1, source_target_pairs={{0,256},{1,769},{2,258},{3,771},{4,260},{5,773},{6,262},{7,775},{8... | collective-permute-start | bytes 1228808 | tf_op jit(solution)/shard_map/ppermute | solution.py:489
  169.2 38.0 %collective-permute-start.18 = (f32[25,2,16,128]{3,2,1,0:T(8,128)S(1)}, f32[25,2,16,128]{3,2,1,0:T(8,128)S(1)}, u32[]{:S(2)}, u32[]{:S(2)}) collective-permute-start(f32[25,2,16,128]{3,2,1,0:T(8,128)S(1)} %collective-permute-done.14.refs_0_), channel_id=1, source_target_pairs={{0,64},{1,193},{2,66},{3,195},{4,68},{5,197},{6,70},{7,199},{8,72}... | collective-permute-start | bytes 1228808 | tf_op jit(solution)/shard_map/ppermute | solution.py:488
  176.8 30.5 %collective-permute-start.21 = (f32[25,2,16,128]{3,2,1,0:T(8,128)S(1)}, f32[25,2,16,128]{3,2,1,0:T(8,128)S(1)}, u32[]{:S(2)}, u32[]{:S(2)}) collective-permute-start(f32[25,2,16,128]{3,2,1,0:T(8,128)S(1)} %collective-permute-done.14.refs_0_), channel_id=1, source_target_pairs={{0,768},{1,257},{2,770},{3,259},{4,772},{5,261},{6,774},{7,263},{8... | collective-permute-start | bytes 1228808 | tf_op jit(solution)/shard_map/ppermute | solution.py:490
  181.2 26.1 %collective-permute-start.20 = (f32[25,2,16,128]{3,2,1,0:T(8,128)S(1)}, f32[25,2,16,128]{3,2,1,0:T(8,128)S(1)}, u32[]{:S(2)}, u32[]{:S(2)}) collective-permute-start(f32[25,2,16,128]{3,2,1,0:T(8,128)S(1)} %collective-permute-done.19.refs_1_), channel_id=1, source_target_pairs={{0,256},{1,769},{2,258},{3,771},{4,260},{5,773},{6,262},{7,775},{8... | collective-permute-start | bytes 1228808 | tf_op jit(solution)/shard_map/ppermute | solution.py:491
  207.3 11.0 %collective-permute-start.22 = (f32[25,2,16,128]{3,2,1,0:T(8,128)S(1)}, f32[25,2,16,128]{3,2,1,0:T(8,128)S(1)}, u32[]{:S(2)}, u32[]{:S(2)}) collective-permute-start(f32[25,2,16,128]{3,2,1,0:T(8,128)S(1)} %collective-permute-done.18.refs_0_), channel_id=1, source_target_pairs={{0,256},{1,769},{2,258},{3,771},{4,260},{5,773},{6,262},{7,775},{8... | collective-permute-start | bytes 1228808 | tf_op jit(solution)/shard_map/ppermute | solution.py:489
  210.7 14.5 %collective-permute-start.24 = (f32[25,2,16,128]{3,2,1,0:T(8,128)S(1)}, f32[25,2,16,128]{3,2,1,0:T(8,128)S(1)}, u32[]{:S(2)}, u32[]{:S(2)}) collective-permute-start(f32[25,2,16,128]{3,2,1,0:T(8,128)S(1)} %collective-permute-done.18.refs_0_), channel_id=1, source_target_pairs={{0,768},{1,257},{2,770},{3,259},{4,772},{5,261},{6,774},{7,263},{8... | collective-permute-start | bytes 1228808 | tf_op jit(solution)/shard_map/ppermute | solution.py:490
  218.3 11.0 %collective-permute-start.23 = (f32[25,2,16,128]{3,2,1,0:T(8,128)S(1)}, f32[25,2,16,128]{3,2,1,0:T(8,128)S(1)}, u32[]{:S(2)}, u32[]{:S(2)}) collective-permute-start(f32[25,2,16,128]{3,2,1,0:T(8,128)S(1)} %collective-permute-done.22.refs_1_), channel_id=1, source_target_pairs={{0,256},{1,769},{2,258},{3,771},{4,260},{5,773},{6,262},{7,775},{8... | collective-permute-start | bytes 1228808 | tf_op jit(solution)/shard_map/ppermute | solution.py:491
  (5 other events, 9.5 us)

commit v4 on v3

--- a/solution.py
+++ b/solution.py
@@ -103,9 +103,9 @@
     corner_left,
     corner_right,
     base,
-    accum,
     next_section,
-    next_accum,
+    held,
+    rates,
     ext,
     side,
     cross_x,
@@ -164,15 +164,13 @@
     lax.fori_loop(0, 30, tilt, 0)
 
     def tile_rates(number, carry):
-        write_rates(
-            number, side, base, accum, next_section, next_accum, ext, cross_x, cross_y
-        )
+        write_rates(number, side, base, next_section, held, rates, ext, cross_x, cross_y)
         return carry
 
     lax.fori_loop(0, planes * rows // TILE, tile_rates, 0)
 
 
-def write_rates(number, side, base, accum, next_section, next_accum, ext, cross_x, cross_y):
+def write_rates(number, side, base, next_section, held, rates_out, ext, cross_x, cross_y):
     parts = 16 // TILE
     plane = number // parts
     start = 0 if parts == 1 else pl.multiple_of((number % parts) * TILE, TILE)
@@ -218,12 +216,14 @@
     rates = evolve_rate(centre, gradients, curves, mixed_terms)
     for field in range(25):
         rate = rates[field] + (-DISSIPATE / 16.0) * smoothing[field]
-        next_section[field, plane, span(0), :] = (
-            base[field, plane, span(0), :] + (0.5 * STEP_DT) * rate
-        )
-        next_accum[field, plane, span(0), :] = (
-            accum[field, plane, span(0), :] + (STEP_DT / 3.0) * rate
-        )
+        result = base[field, plane, span(0), :] + (0.5 * STEP_DT) * rate
+        next_section[field, plane, span(0), :] = result
+        held[field, plane, span(0), :] = result
+        rates_out[field, plane, span(0), :] = rate
+
+
+def tally_kernel(accum, rates, next_accum):
+    next_accum[...] = accum[...] + (STEP_DT / 3.0) * rates[...]
 
 
 def evolve_rate(centre, gradients, curves, mixed_terms):
@@ -544,11 +544,11 @@
     edges_above = sent(edges, "gz", -1)
     corner_left = sent(right, "gx", 1)
     corner_right = sent(left, "gx", -1)
-    next_section, next_accum = pl.pallas_call(
+    next_section, result, rates = pl.pallas_call(
         rate_kernel,
-        out_shape=(block, block),
-        in_specs=vmem(13),
-        out_specs=tuple(vmem(2)),
+        out_shape=(block, block, block),
+        in_specs=vmem(12),
+        out_specs=tuple(vmem(3)),
         scratch_shapes=[
             pltpu.VMEM((25, 6, 32, 128), jnp.float32),
             pltpu.VMEM((25, 2, 16, 128), jnp.float32),
@@ -571,9 +571,17 @@
         corner_left,
         corner_right,
         base,
-        accum,
-    )
-    return (next_section, next_accum, slab_of(next_section))
+    )
+    next_accum = pl.pallas_call(
+        tally_kernel,
+        out_shape=block,
+        in_specs=vmem(2),
+        out_specs=vmem(1)[0],
+        compiler_params=pltpu.CompilerParams(vmem_limit_bytes=4 * 1024 * 1024),
+        cost_estimate=pl.CostEstimate(flops=200000, bytes_accessed=1300000, transcendentals=0),
+        name="tally",
+    )(accum, rates)
+    return (next_section, next_accum, slab_of(result))
 
 
 def solution(mesh):

time: 232 us -> 230 us (level)
    pallas_call x1 -> x2, Pallas kernels: 6.02 us -> 6.65 us  [the longest x1 5.83 us: shards(): pl.pallas_call(rate_kernel, out_shape=(block, block, block), in_specs=vme...]
where the time goes in v4:
time: 230 us; the launch traced here: 229 us
  starting transfers between devices  124 us (54%)
  waiting for transfers between devices  89.4 us (39%)
  Pallas kernels  11.8 us (5%)
  local copies, waits for them, and re-layouts  3 us (1%)
    ppermute x3, waiting for transfers between devices, slab_of(): following = lax.ppermute(current, AXES, along_y)  70.7 us
    ppermute x10, starting transfers between devices, sent(): return lax.ppermute(array, axis, ring(axis, step))  48.3 us
    ppermute x3, starting transfers between devices, slab_of(): following = lax.ppermute(current, AXES, along_y)  35.1 us
    ppermute x4, starting transfers between devices, slab_of(): back = lax.ppermute(current, AXES, against_x)  17.7 us
    ppermute x4, starting transfers between devices, slab_of(): second = lax.ppermute(first, AXES, along_x)  11.5 us
    ppermute x4, starting transfers between devices, slab_of(): first = lax.ppermute(current, AXES, along_x)  11.4 us
    ppermute x10, waiting for transfers between devices, sent(): return lax.ppermute(array, axis, ring(axis, step))  11.3 us
    pallas_call x1, Pallas kernels, shards(): pl.pallas_call(rate_kernel, out_shape=(block, block, block), in_specs=vme...  5.83 us
  transfers between devices with their start and end apart: 25, of which 9 were waited for; matrix products, arithmetic and copies ran while one was open for 0% of the time, Pallas kernels for 2%

profile of v4, /device:TPU:38, one launch (start us, length us, event | category | flops | bytes accessed | tf_op | source)
XLA Modules:
  0.0 229.2 jit_solution(13303192001373735792)
XLA Ops:
  2.6 3.6 %collective-permute-start.1 = (f32[25,2,16,128]{3,2,1,0:T(8,128)}, f32[25,2,16,128]{3,2,1,0:T(8,128)S(1)}, u32[]{:S(2)}, u32[]{:S(2)}) collective-permute-start(f32[25,2,16,128]{3,2,1,0:T(8,128)} %section.1), channel_id=1, source_target_pairs={{0,63},{1,0},{2,1},{3,2},{4,3},{5,4},{6,5},{7,6},{8,7},{9,8},{10,9... | collective-permute-start | bytes 1228808 | tf_op jit(solution)/shard_map/ppermute | solution.py:507
  7.5 15.7 %collective-permute-start.4 = (f32[100,128]{1,0:T(8,128)S(1)}, f32[100,128]{1,0:T(8,128)S(1)}, u32[]{:S(2)}, u32[]{:S(2)}) collective-permute-start(f32[100,128]{1,0:T(8,128)S(1)} %get-tuple-element.29), channel_id=1, source_target_pairs={{0,64},{64,128},{128,192},{192,0},{1,65},{65,129},{129,193},{193,1... | collective-permute-start | bytes 153608 | tf_op jit(solution)/shard_map/ppermute | solution.py:507
  23.2 8.3 %collective-permute-start.5 = (f32[100,128]{1,0:T(8,128)S(1)}, f32[100,128]{1,0:T(8,128)S(1)}, u32[]{:S(2)}, u32[]{:S(2)}) collective-permute-start(f32[100,128]{1,0:T(8,128)S(1)} %get-tuple-element.30), channel_id=1, source_target_pairs={{0,192},{64,0},{128,64},{192,128},{1,193},{65,1},{129,65},{193,129... | collective-permute-start | bytes 153608 | tf_op jit(solution)/shard_map/ppermute | solution.py:507
  31.5 3.5 %collective-permute-start.2 = (f32[16,128]{1,0:T(8,128)S(1)}, f32[16,128]{1,0:T(8,128)S(1)}, u32[]{:S(2)}, u32[]{:S(2)}) collective-permute-start(f32[16,128]{1,0:T(8,128)S(1)} %get-tuple-element.27), channel_id=1, source_target_pairs={{0,256},{256,512},{512,768},{768,0},{1,257},{257,513},{513,769},{7... | collective-permute-start | bytes 24584 | tf_op jit(solution)/shard_map/ppermute | solution.py:507
  35.0 3.3 %collective-permute-done.2.from_left = f32[16,128]{1,0:T(8,128)S(1)} collective-permute-done((f32[16,128]{1,0:T(8,128)S(1)}, f32[16,128]{1,0:T(8,128)S(1)}, u32[]{:S(2)}, u32[]{:S(2)}) %collective-permute-start.2) | collective-permute-done | bytes 8224 | tf_op jit(solution)/shard_map/ppermute | solution.py:507
  38.3 3.7 %collective-permute-start.3 = (f32[16,128]{1,0:T(8,128)S(1)}, f32[16,128]{1,0:T(8,128)S(1)}, u32[]{:S(2)}, u32[]{:S(2)}) collective-permute-start(f32[16,128]{1,0:T(8,128)S(1)} %get-tuple-element.28), channel_id=1, source_target_pairs={{0,768},{256,0},{512,256},{768,512},{1,769},{257,1},{513,257},{769... | collective-permute-start | bytes 24584 | tf_op jit(solution)/shard_map/ppermute | solution.py:507
  45.9 3.6 %collective-permute-start.7 = (f32[72,128]{1,0:T(8,128)S(1)}, f32[72,128]{1,0:T(8,128)S(1)}, u32[]{:S(2)}, u32[]{:S(2)}) collective-permute-start(f32[72,128]{1,0:T(8,128)S(1)} %get-tuple-element.31), channel_id=1, source_target_pairs={{0,63},{1,0},{2,1},{3,2},{4,3},{5,4},{6,5},{7,6},{8,7},{9,8},{10,9... | collective-permute-start | bytes 110600 | tf_op jit(solution)/shard_map/ppermute | solution.py:507
  51.8 4.4 %collective-permute-done.8.corner_left = f32[4,128]{1,0:T(4,128)S(1)} collective-permute-done((f32[4,128]{1,0:T(4,128)S(1)}, f32[4,128]{1,0:T(4,128)S(1)}, u32[]{:S(2)}, u32[]{:S(2)}) %collective-permute-start.8) | collective-permute-done | bytes 2080 | tf_op jit(solution)/shard_map/ppermute | solution.py:507
  56.2 3.7 %collective-permute-start.9 = (f32[4,128]{1,0:T(4,128)S(1)}, f32[4,128]{1,0:T(4,128)S(1)}, u32[]{:S(2)}, u32[]{:S(2)}) collective-permute-start(f32[4,128]{1,0:T(4,128)S(1)} %get-tuple-element.33), channel_id=1, source_target_pairs={{0,768},{256,0},{512,256},{768,512},{1,769},{257,1},{513,257},{769... | collective-permute-start | bytes 6152 | tf_op jit(solution)/shard_map/ppermute | solution.py:507
  62.7 5.8 %rate.1 = (f32[25,2,16,128]{3,2,1,0:T(8,128)}, f32[25,2,16,128]{3,2,1,0:T(8,128)S(1)}, f32[25,2,16,128]{3,2,1,0:T(8,128)S(1)}) custom-call(f32[25,2,16,128]{3,2,1,0:T(8,128)S(1)} %get-tuple-element.26.section, f32[25,2,16,128]{3,2,1,0:T(8,128)S(1)} %collective-permute-done.below, f32[25,2,16,128]{3,2,1,0:T(8,128)S(1)} %collective-permute-done.1.above, ...), custom_call_target="tpu_custom_call" | custom-call | flops 30000000 | bytes 3000000 | tf_op jit(solution)/shard_map/rate/pallas_call | solution.py:547
  70.5 14.4 %collective-permute-start.10 = (f32[25,2,16,128]{3,2,1,0:T(8,128)S(1)}, f32[25,2,16,128]{3,2,1,0:T(8,128)S(1)}, u32[]{:S(2)}, u32[]{:S(2)}) collective-permute-start(f32[25,2,16,128]{3,2,1,0:T(8,128)S(1)} %get-tuple-element.36.refs_0_), channel_id=1, source_target_pairs={{0,64},{1,193},{2,66},{3,195},{4,68},{5,197},{6,70},{7,199},{8,72}... | collective-permute-start | bytes 1228808 | tf_op jit(solution)/shard_map/ppermute | solution.py:488
  84.9 4.8 %collective-permute-start.13 = (f32[25,2,16,128]{3,2,1,0:T(8,128)S(1)}, f32[25,2,16,128]{3,2,1,0:T(8,128)S(1)}, u32[]{:S(2)}, u32[]{:S(2)}) collective-permute-start(f32[25,2,16,128]{3,2,1,0:T(8,128)S(1)} %get-tuple-element.36.refs_0_), channel_id=1, source_target_pairs={{0,768},{1,257},{2,770},{3,259},{4,772},{5,261},{6,774},{7,263},{8... | collective-permute-start | bytes 1228808 | tf_op jit(solution)/shard_map/ppermute | solution.py:490
  91.6 27.1 %collective-permute-done.10.refs_0_ = f32[25,2,16,128]{3,2,1,0:T(8,128)S(1)} collective-permute-done((f32[25,2,16,128]{3,2,1,0:T(8,128)S(1)}, f32[25,2,16,128]{3,2,1,0:T(8,128)S(1)}, u32[]{:S(2)}, u32[]{:S(2)}) %collective-permute-start.10) | collective-permute-done | bytes 409632 | tf_op jit(solution)/shard_map/ppermute | solution.py:488
  121.7 13.2 %collective-permute-start.14 = (f32[25,2,16,128]{3,2,1,0:T(8,128)S(1)}, f32[25,2,16,128]{3,2,1,0:T(8,128)S(1)}, u32[]{:S(2)}, u32[]{:S(2)}) collective-permute-start(f32[25,2,16,128]{3,2,1,0:T(8,128)S(1)} %collective-permute-done.10.refs_0_), channel_id=1, source_target_pairs={{0,64},{1,193},{2,66},{3,195},{4,68},{5,197},{6,70},{7,199},{8,72}... | collective-permute-start | bytes 1228808 | tf_op jit(solution)/shard_map/ppermute | solution.py:488
  134.9 4.8 %collective-permute-start.17 = (f32[25,2,16,128]{3,2,1,0:T(8,128)S(1)}, f32[25,2,16,128]{3,2,1,0:T(8,128)S(1)}, u32[]{:S(2)}, u32[]{:S(2)}) collective-permute-start(f32[25,2,16,128]{3,2,1,0:T(8,128)S(1)} %collective-permute-done.10.refs_0_), channel_id=1, source_target_pairs={{0,768},{1,257},{2,770},{3,259},{4,772},{5,261},{6,774},{7,263},{8... | collective-permute-start | bytes 1228808 | tf_op jit(solution)/shard_map/ppermute | solution.py:490
  142.9 21.8 %collective-permute-done.14.refs_0_ = f32[25,2,16,128]{3,2,1,0:T(8,128)S(1)} collective-permute-done((f32[25,2,16,128]{3,2,1,0:T(8,128)S(1)}, f32[25,2,16,128]{3,2,1,0:T(8,128)S(1)}, u32[]{:S(2)}, u32[]{:S(2)}) %collective-permute-start.14) | collective-permute-done | bytes 409632 | tf_op jit(solution)/shard_map/ppermute | solution.py:488
  167.8 7.5 %collective-permute-start.18 = (f32[25,2,16,128]{3,2,1,0:T(8,128)S(1)}, f32[25,2,16,128]{3,2,1,0:T(8,128)S(1)}, u32[]{:S(2)}, u32[]{:S(2)}) collective-permute-start(f32[25,2,16,128]{3,2,1,0:T(8,128)S(1)} %collective-permute-done.14.refs_0_), channel_id=1, source_target_pairs={{0,64},{1,193},{2,66},{3,195},{4,68},{5,197},{6,70},{7,199},{8,72}... | collective-permute-start | bytes 1228808 | tf_op jit(solution)/shard_map/ppermute | solution.py:488
  175.4 4.4 %collective-permute-start.21 = (f32[25,2,16,128]{3,2,1,0:T(8,128)S(1)}, f32[25,2,16,128]{3,2,1,0:T(8,128)S(1)}, u32[]{:S(2)}, u32[]{:S(2)}) collective-permute-start(f32[25,2,16,128]{3,2,1,0:T(8,128)S(1)} %collective-permute-done.14.refs_0_), channel_id=1, source_target_pairs={{0,768},{1,257},{2,770},{3,259},{4,772},{5,261},{6,774},{7,263},{8... | collective-permute-start | bytes 1228808 | tf_op jit(solution)/shard_map/ppermute | solution.py:490
  179.9 4.2 %collective-permute-start.20 = (f32[25,2,16,128]{3,2,1,0:T(8,128)S(1)}, f32[25,2,16,128]{3,2,1,0:T(8,128)S(1)}, u32[]{:S(2)}, u32[]{:S(2)}) collective-permute-start(f32[25,2,16,128]{3,2,1,0:T(8,128)S(1)} %collective-permute-done.19.refs_1_), channel_id=1, source_target_pairs={{0,256},{1,769},{2,258},{3,771},{4,260},{5,773},{6,262},{7,775},{8... | collective-permute-start | bytes 1228808 | tf_op jit(solution)/shard_map/ppermute | solution.py:491
  184.1 21.8 %collective-permute-done.18.refs_0_ = f32[25,2,16,128]{3,2,1,0:T(8,128)S(1)} collective-permute-done((f32[25,2,16,128]{3,2,1,0:T(8,128)S(1)}, f32[25,2,16,128]{3,2,1,0:T(8,128)S(1)}, u32[]{:S(2)}, u32[]{:S(2)}) %collective-permute-start.18) | collective-permute-done | bytes 409632 | tf_op jit(solution)/shard_map/ppermute | solution.py:488
  205.9 3.4 %collective-permute-start.22 = (f32[25,2,16,128]{3,2,1,0:T(8,128)S(1)}, f32[25,2,16,128]{3,2,1,0:T(8,128)S(1)}, u32[]{:S(2)}, u32[]{:S(2)}) collective-permute-start(f32[25,2,16,128]{3,2,1,0:T(8,128)S(1)} %collective-permute-done.18.refs_0_), channel_id=1, source_target_pairs={{0,256},{1,769},{2,258},{3,771},{4,260},{5,773},{6,262},{7,775},{8... | collective-permute-start | bytes 1228808 | tf_op jit(solution)/shard_map/ppermute | solution.py:489
  209.3 3.6 %collective-permute-start.24 = (f32[25,2,16,128]{3,2,1,0:T(8,128)S(1)}, f32[25,2,16,128]{3,2,1,0:T(8,128)S(1)}, u32[]{:S(2)}, u32[]{:S(2)}) collective-permute-start(f32[25,2,16,128]{3,2,1,0:T(8,128)S(1)} %collective-permute-done.18.refs_0_), channel_id=1, source_target_pairs={{0,768},{1,257},{2,770},{3,259},{4,772},{5,261},{6,774},{7,263},{8... | collective-permute-start | bytes 1228808 | tf_op jit(solution)/shard_map/ppermute | solution.py:490
  213.0 4.0 %collective-permute-done.22.refs_1_ = f32[25,2,16,128]{3,2,1,0:T(8,128)S(1)} collective-permute-done((f32[25,2,16,128]{3,2,1,0:T(8,128)S(1)}, f32[25,2,16,128]{3,2,1,0:T(8,128)S(1)}, u32[]{:S(2)}, u32[]{:S(2)}) %collective-permute-start.22) | collective-permute-done | bytes 409632 | tf_op jit(solution)/shard_map/ppermute | solution.py:489
  224.6 3.4 %collective-permute-done.23.refs_2_ = f32[25,2,16,128]{3,2,1,0:T(8,128)S(1)} collective-permute-done((f32[25,2,16,128]{3,2,1,0:T(8,128)S(1)}, f32[25,2,16,128]{3,2,1,0:T(8,128)S(1)}, u32[]{:S(2)}, u32[]{:S(2)}) %collective-permute-start.23) | collective-permute-done | bytes 409632 | tf_op jit(solution)/shard_map/ppermute | solution.py:491
  (40 shorter events, 34.0 us)
Async XLA Ops:
  0.6 61.1 %collective-permute-start = (f32[25,2,16,128]{3,2,1,0:T(8,128)}, f32[25,2,16,128]{3,2,1,0:T(8,128)S(1)}, u32[]{:S(2)}, u32[]{:S(2)}) collective-permute-start(f32[25,2,16,128]{3,2,1,0:T(8,128)} %section.1), channel_id=1, source_target_pairs={{0,1},{1,2},{2,3},{3,4},{4,5},{5,6},{6,7},{7,8},{8,9},{9,10},{10,1... | collective-permute-start | bytes 1228808 | tf_op jit(solution)/shard_map/ppermute | solution.py:507
  2.6 59.1 %collective-permute-start.1 = (f32[25,2,16,128]{3,2,1,0:T(8,128)}, f32[25,2,16,128]{3,2,1,0:T(8,128)S(1)}, u32[]{:S(2)}, u32[]{:S(2)}) collective-permute-start(f32[25,2,16,128]{3,2,1,0:T(8,128)} %section.1), channel_id=1, source_target_pairs={{0,63},{1,0},{2,1},{3,2},{4,3},{5,4},{6,5},{7,6},{8,7},{9,8},{10,9... | collective-permute-start | bytes 1228808 | tf_op jit(solution)/shard_map/ppermute | solution.py:507
  7.5 36.3 %collective-permute-start.4 = (f32[100,128]{1,0:T(8,128)S(1)}, f32[100,128]{1,0:T(8,128)S(1)}, u32[]{:S(2)}, u32[]{:S(2)}) collective-permute-start(f32[100,128]{1,0:T(8,128)S(1)} %get-tuple-element.29), channel_id=1, source_target_pairs={{0,64},{64,128},{128,192},{192,0},{1,65},{65,129},{129,193},{193,1... | collective-permute-start | bytes 153608 | tf_op jit(solution)/shard_map/ppermute | solution.py:507
  23.2 20.6 %collective-permute-start.5 = (f32[100,128]{1,0:T(8,128)S(1)}, f32[100,128]{1,0:T(8,128)S(1)}, u32[]{:S(2)}, u32[]{:S(2)}) collective-permute-start(f32[100,128]{1,0:T(8,128)S(1)} %get-tuple-element.30), channel_id=1, source_target_pairs={{0,192},{64,0},{128,64},{192,128},{1,193},{65,1},{129,65},{193,129... | collective-permute-start | bytes 153608 | tf_op jit(solution)/shard_map/ppermute | solution.py:507
  31.5 6.8 %collective-permute-start.2 = (f32[16,128]{1,0:T(8,128)S(1)}, f32[16,128]{1,0:T(8,128)S(1)}, u32[]{:S(2)}, u32[]{:S(2)}) collective-permute-start(f32[16,128]{1,0:T(8,128)S(1)} %get-tuple-element.27), channel_id=1, source_target_pairs={{0,256},{256,512},{512,768},{768,0},{1,257},{257,513},{513,769},{7... | collective-permute-start | bytes 24584 | tf_op jit(solution)/shard_map/ppermute | solution.py:507
  38.3 5.5 %collective-permute-start.3 = (f32[16,128]{1,0:T(8,128)S(1)}, f32[16,128]{1,0:T(8,128)S(1)}, u32[]{:S(2)}, u32[]{:S(2)}) collective-permute-start(f32[16,128]{1,0:T(8,128)S(1)} %get-tuple-element.28), channel_id=1, source_target_pairs={{0,768},{256,0},{512,256},{768,512},{1,769},{257,1},{513,257},{769... | collective-permute-start | bytes 24584 | tf_op jit(solution)/shard_map/ppermute | solution.py:507
  43.9 17.7 %collective-permute-start.6 = (f32[72,128]{1,0:T(8,128)S(1)}, f32[72,128]{1,0:T(8,128)S(1)}, u32[]{:S(2)}, u32[]{:S(2)}) collective-permute-start(f32[72,128]{1,0:T(8,128)S(1)} %get-tuple-element.31), channel_id=1, source_target_pairs={{0,1},{1,2},{2,3},{3,4},{4,5},{5,6},{6,7},{7,8},{8,9},{9,10},{10,1... | collective-permute-start | bytes 110600 | tf_op jit(solution)/shard_map/ppermute | solution.py:507
  45.9 15.8 %collective-permute-start.7 = (f32[72,128]{1,0:T(8,128)S(1)}, f32[72,128]{1,0:T(8,128)S(1)}, u32[]{:S(2)}, u32[]{:S(2)}) collective-permute-start(f32[72,128]{1,0:T(8,128)S(1)} %get-tuple-element.31), channel_id=1, source_target_pairs={{0,63},{1,0},{2,1},{3,2},{4,3},{5,4},{6,5},{7,6},{8,7},{9,8},{10,9... | collective-permute-start | bytes 110600 | tf_op jit(solution)/shard_map/ppermute | solution.py:507
  49.5 6.7 %collective-permute-start.8 = (f32[4,128]{1,0:T(4,128)S(1)}, f32[4,128]{1,0:T(4,128)S(1)}, u32[]{:S(2)}, u32[]{:S(2)}) collective-permute-start(f32[4,128]{1,0:T(4,128)S(1)} %get-tuple-element.32), channel_id=1, source_target_pairs={{0,256},{256,512},{512,768},{768,0},{1,257},{257,513},{513,769},{7... | collective-permute-start | bytes 6152 | tf_op jit(solution)/shard_map/ppermute | solution.py:507
  68.5 21.1 %collective-permute-start.11 = (f32[25,2,16,128]{3,2,1,0:T(8,128)S(1)}, f32[25,2,16,128]{3,2,1,0:T(8,128)S(1)}, u32[]{:S(2)}, u32[]{:S(2)}) collective-permute-start(f32[25,2,16,128]{3,2,1,0:T(8,128)S(1)} %get-tuple-element.36.refs_0_), channel_id=1, source_target_pairs={{0,256},{1,769},{2,258},{3,771},{4,260},{5,773},{6,262},{7,775},{8... | collective-permute-start | bytes 1228808 | tf_op jit(solution)/shard_map/ppermute | solution.py:489
  70.5 48.3 %collective-permute-start.10 = (f32[25,2,16,128]{3,2,1,0:T(8,128)S(1)}, f32[25,2,16,128]{3,2,1,0:T(8,128)S(1)}, u32[]{:S(2)}, u32[]{:S(2)}) collective-permute-start(f32[25,2,16,128]{3,2,1,0:T(8,128)S(1)} %get-tuple-element.36.refs_0_), channel_id=1, source_target_pairs={{0,64},{1,193},{2,66},{3,195},{4,68},{5,197},{6,70},{7,199},{8,72}... | collective-permute-start | bytes 1228808 | tf_op jit(solution)/shard_map/ppermute | solution.py:488
  84.9 33.8 %collective-permute-start.13 = (f32[25,2,16,128]{3,2,1,0:T(8,128)S(1)}, f32[25,2,16,128]{3,2,1,0:T(8,128)S(1)}, u32[]{:S(2)}, u32[]{:S(2)}) collective-permute-start(f32[25,2,16,128]{3,2,1,0:T(8,128)S(1)} %get-tuple-element.36.refs_0_), channel_id=1, source_target_pairs={{0,768},{1,257},{2,770},{3,259},{4,772},{5,261},{6,774},{7,263},{8... | collective-permute-start | bytes 1228808 | tf_op jit(solution)/shard_map/ppermute | solution.py:490
  89.7 29.0 %collective-permute-start.12 = (f32[25,2,16,128]{3,2,1,0:T(8,128)S(1)}, f32[25,2,16,128]{3,2,1,0:T(8,128)S(1)}, u32[]{:S(2)}, u32[]{:S(2)}) collective-permute-start(f32[25,2,16,128]{3,2,1,0:T(8,128)S(1)} %collective-permute-done.11.refs_1_), channel_id=1, source_target_pairs={{0,256},{1,769},{2,258},{3,771},{4,260},{5,773},{6,262},{7,775},{8... | collective-permute-start | bytes 1228808 | tf_op jit(solution)/shard_map/ppermute | solution.py:491
  118.7 21.0 %collective-permute-start.15 = (f32[25,2,16,128]{3,2,1,0:T(8,128)S(1)}, f32[25,2,16,128]{3,2,1,0:T(8,128)S(1)}, u32[]{:S(2)}, u32[]{:S(2)}) collective-permute-start(f32[25,2,16,128]{3,2,1,0:T(8,128)S(1)} %collective-permute-done.10.refs_0_), channel_id=1, source_target_pairs={{0,256},{1,769},{2,258},{3,771},{4,260},{5,773},{6,262},{7,775},{8... | collective-permute-start | bytes 1228808 | tf_op jit(solution)/shard_map/ppermute | solution.py:489
  121.7 43.0 %collective-permute-start.14 = (f32[25,2,16,128]{3,2,1,0:T(8,128)S(1)}, f32[25,2,16,128]{3,2,1,0:T(8,128)S(1)}, u32[]{:S(2)}, u32[]{:S(2)}) collective-permute-start(f32[25,2,16,128]{3,2,1,0:T(8,128)S(1)} %collective-permute-done.10.refs_0_), channel_id=1, source_target_pairs={{0,64},{1,193},{2,66},{3,195},{4,68},{5,197},{6,70},{7,199},{8,72}... | collective-permute-start | bytes 1228808 | tf_op jit(solution)/shard_map/ppermute | solution.py:488
  134.9 29.9 %collective-permute-start.17 = (f32[25,2,16,128]{3,2,1,0:T(8,128)S(1)}, f32[25,2,16,128]{3,2,1,0:T(8,128)S(1)}, u32[]{:S(2)}, u32[]{:S(2)}) collective-permute-start(f32[25,2,16,128]{3,2,1,0:T(8,128)S(1)} %collective-permute-done.10.refs_0_), channel_id=1, source_target_pairs={{0,768},{1,257},{2,770},{3,259},{4,772},{5,261},{6,774},{7,263},{8... | collective-permute-start | bytes 1228808 | tf_op jit(solution)/shard_map/ppermute | solution.py:490
  139.8 25.0 %collective-permute-start.16 = (f32[25,2,16,128]{3,2,1,0:T(8,128)S(1)}, f32[25,2,16,128]{3,2,1,0:T(8,128)S(1)}, u32[]{:S(2)}, u32[]{:S(2)}) collective-permute-start(f32[25,2,16,128]{3,2,1,0:T(8,128)S(1)} %collective-permute-done.15.refs_1_), channel_id=1, source_target_pairs={{0,256},{1,769},{2,258},{3,771},{4,260},{5,773},{6,262},{7,775},{8... | collective-permute-start | bytes 1228808 | tf_op jit(solution)/shard_map/ppermute | solution.py:491
  164.8 15.1 %collective-permute-start.19 = (f32[25,2,16,128]{3,2,1,0:T(8,128)S(1)}, f32[25,2,16,128]{3,2,1,0:T(8,128)S(1)}, u32[]{:S(2)}, u32[]{:S(2)}) collective-permute-start(f32[25,2,16,128]{3,2,1,0:T(8,128)S(1)} %collective-permute-done.14.refs_0_), channel_id=1, source_target_pairs={{0,256},{1,769},{2,258},{3,771},{4,260},{5,773},{6,262},{7,775},{8... | collective-permute-start | bytes 1228808 | tf_op jit(solution)/shard_map/ppermute | solution.py:489
  167.8 38.0 %collective-permute-start.18 = (f32[25,2,16,128]{3,2,1,0:T(8,128)S(1)}, f32[25,2,16,128]{3,2,1,0:T(8,128)S(1)}, u32[]{:S(2)}, u32[]{:S(2)}) collective-permute-start(f32[25,2,16,128]{3,2,1,0:T(8,128)S(1)} %collective-permute-done.14.refs_0_), channel_id=1, source_target_pairs={{0,64},{1,193},{2,66},{3,195},{4,68},{5,197},{6,70},{7,199},{8,72}... | collective-permute-start | bytes 1228808 | tf_op jit(solution)/shard_map/ppermute | solution.py:488
  175.4 30.5 %collective-permute-start.21 = (f32[25,2,16,128]{3,2,1,0:T(8,128)S(1)}, f32[25,2,16,128]{3,2,1,0:T(8,128)S(1)}, u32[]{:S(2)}, u32[]{:S(2)}) collective-permute-start(f32[25,2,16,128]{3,2,1,0:T(8,128)S(1)} %collective-permute-done.14.refs_0_), channel_id=1, source_target_pairs={{0,768},{1,257},{2,770},{3,259},{4,772},{5,261},{6,774},{7,263},{8... | collective-permute-start | bytes 1228808 | tf_op jit(solution)/shard_map/ppermute | solution.py:490
  179.9 26.0 %collective-permute-start.20 = (f32[25,2,16,128]{3,2,1,0:T(8,128)S(1)}, f32[25,2,16,128]{3,2,1,0:T(8,128)S(1)}, u32[]{:S(2)}, u32[]{:S(2)}) collective-permute-start(f32[25,2,16,128]{3,2,1,0:T(8,128)S(1)} %collective-permute-done.19.refs_1_), channel_id=1, source_target_pairs={{0,256},{1,769},{2,258},{3,771},{4,260},{5,773},{6,262},{7,775},{8... | collective-permute-start | bytes 1228808 | tf_op jit(solution)/shard_map/ppermute | solution.py:491
  205.9 11.0 %collective-permute-start.22 = (f32[25,2,16,128]{3,2,1,0:T(8,128)S(1)}, f32[25,2,16,128]{3,2,1,0:T(8,128)S(1)}, u32[]{:S(2)}, u32[]{:S(2)}) collective-permute-start(f32[25,2,16,128]{3,2,1,0:T(8,128)S(1)} %collective-permute-done.18.refs_0_), channel_id=1, source_target_pairs={{0,256},{1,769},{2,258},{3,771},{4,260},{5,773},{6,262},{7,775},{8... | collective-permute-start | bytes 1228808 | tf_op jit(solution)/shard_map/ppermute | solution.py:489
  209.3 15.3 %collective-permute-start.24 = (f32[25,2,16,128]{3,2,1,0:T(8,128)S(1)}, f32[25,2,16,128]{3,2,1,0:T(8,128)S(1)}, u32[]{:S(2)}, u32[]{:S(2)}) collective-permute-start(f32[25,2,16,128]{3,2,1,0:T(8,128)S(1)} %collective-permute-done.18.refs_0_), channel_id=1, source_target_pairs={{0,768},{1,257},{2,770},{3,259},{4,772},{5,261},{6,774},{7,263},{8... | collective-permute-start | bytes 1228808 | tf_op jit(solution)/shard_map/ppermute | solution.py:490
  216.9 11.0 %collective-permute-start.23 = (f32[25,2,16,128]{3,2,1,0:T(8,128)S(1)}, f32[25,2,16,128]{3,2,1,0:T(8,128)S(1)}, u32[]{:S(2)}, u32[]{:S(2)}) collective-permute-start(f32[25,2,16,128]{3,2,1,0:T(8,128)S(1)} %collective-permute-done.22.refs_1_), channel_id=1, source_target_pairs={{0,256},{1,769},{2,258},{3,771},{4,260},{5,773},{6,262},{7,775},{8... | collective-permute-start | bytes 1228808 | tf_op jit(solution)/shard_map/ppermute | solution.py:491
  (4 other events, 8.5 us)
